TPU v7x, 64 devices: a 2x2x8 block of a 4x4x8 slice. The times are simulated.
64 devices in a mesh: sys: 4 (over x, y), blk: 16 (over z, core).
Axes of the slice: x: 2, y: 2, z: 8, core: 2. Of those that a mesh axis runs over, the one named last changes fastest.
The devices are a block of a 4x4x8 slice.
Arguments:
- positions: float32 [65536, 256], P(('sys', 'blk')), parts along dimension 0
- velocity: float32 [65536, 256], P(('sys', 'blk')), parts along dimension 0
- charges: float32 [65536], P(('sys', 'blk')), parts along dimension 0
Outputs:
- output 1: float32 [65536, 256], P(('sys', 'blk')), parts along dimension 0
- output 2: float32 [4], P('sys'), parts along dimension 0
- output 3: float32 [65536, 256], P(('sys', 'blk')), parts along dimension 0
- output 4: float32 [65536, 256], P(('sys', 'blk')), parts along dimension 0
There are 4 independent parts. A program takes and returns all parts, laid end to end along the dimension named above; each array names one.
All inputs are finite; a program needn't handle non-finite values.
Results may differ from a plain program's by a relative error of at most 0.00277111.
Values are sent between devices in bfloat16 or wider.
A program may use at most 768 MiB of HBM per device.

v0:
```python
import jax
import jax.numpy as jnp
from jax import lax
from jax.sharding import PartitionSpec as P

STEP_SIZE = 0.5
ROW_TILE = 256


def block_pair(x_a, q_a, x_b, q_b, same_block, want_b):
    rows_a, feat_dim = x_a.shape
    rows_b = x_b.shape[0]
    ell_sq = 1.0 * feat_dim
    tile_rows = min(rows_a, ROW_TILE)
    sq_a = jnp.sum(jnp.square(x_a.astype(jnp.float32)), axis=1)
    sq_b = jnp.sum(jnp.square(x_b.astype(jnp.float32)), axis=1)
    col_ids = jnp.arange(rows_b)

    def tile_step(state_in, tile_idx):
        col_sum, back_sum, weight_total = state_in
        row_start = tile_idx * tile_rows
        x_tile = lax.dynamic_slice_in_dim(x_a, row_start, tile_rows, 0)
        q_tile = lax.dynamic_slice_in_dim(q_a, row_start, tile_rows, 0)
        sq_tile = lax.dynamic_slice_in_dim(sq_a, row_start, tile_rows, 0)
        gram_tile = jnp.einsum("id,jd->ij", x_tile, x_b, preferred_element_type=jnp.float32)
        dist_sq = jnp.maximum(sq_tile[:, None] + sq_b[None, :] - 2.0 * gram_tile, 0.0)
        weight = q_tile[:, None] * q_b[None, :] * jnp.exp(-dist_sq / (2.0 * ell_sq))
        if same_block:
            on_diag = (row_start + jnp.arange(tile_rows))[:, None] == col_ids[None, :]
            weight = jnp.where(on_diag, 0.0, weight)
        w_low = weight.astype(jnp.bfloat16)
        pull_sum = jnp.dot(w_low, x_b, preferred_element_type=jnp.float32)
        force_tile = jnp.sum(weight, axis=1)[:, None] * x_tile.astype(jnp.float32) - pull_sum
        if want_b:
            col_sum = col_sum + jnp.sum(weight, axis=0)
            back_sum = back_sum + jnp.einsum("ij,id->jd", w_low, x_tile, preferred_element_type=jnp.float32)
        return (col_sum, back_sum, weight_total + jnp.sum(weight)), force_tile

    if want_b:
        start_state = (jnp.zeros((rows_b,), jnp.float32), jnp.zeros((rows_b, feat_dim), jnp.float32), jnp.zeros((), jnp.float32))
    else:
        start_state = (jnp.zeros((), jnp.float32), jnp.zeros((), jnp.float32), jnp.zeros((), jnp.float32))
    end_state, force_tiles = lax.scan(tile_step, start_state, jnp.arange(rows_a // tile_rows))
    col_sum, back_sum, weight_total = end_state
    force_a = force_tiles.reshape(rows_a, feat_dim)
    react_b = col_sum[:, None] * x_b.astype(jnp.float32) - back_sum if want_b else None
    return force_a, react_b, weight_total


def paired_forces(positions, charges, blk_size):
    x_host = positions.astype(jnp.bfloat16)
    host_rows, feat_dim = x_host.shape
    my_index = lax.axis_index("blk")
    half_way = blk_size // 2
    odd_steps = (blk_size - 1) // 2
    next_perm = [(i, (i + 1) % blk_size) for i in range(blk_size)]
    home_perm = [(i, (i - half_way) % blk_size) for i in range(blk_size)]
    force_acc, _, self_sum = block_pair(x_host, charges, x_host, charges, True, False)
    energy_acc = 0.5 * self_sum
    react_acc = jnp.zeros((host_rows, feat_dim), jnp.float32)
    x_vis = x_host
    q_vis = charges
    if odd_steps >= 1:
        x_vis = lax.ppermute(x_host, "blk", next_perm)
        q_vis = lax.ppermute(charges, "blk", next_perm)
        force_new, react_acc, pair_sum = block_pair(x_host, charges, x_vis, q_vis, False, True)
        force_acc = force_acc + force_new
        energy_acc = energy_acc + pair_sum

        def pair_step(step_idx, state_in):
            force_run, energy_run, x_seen, q_seen, react_run = state_in
            x_seen = lax.ppermute(x_seen, "blk", next_perm)
            q_seen = lax.ppermute(q_seen, "blk", next_perm)
            react_run = lax.ppermute(react_run, "blk", next_perm)
            force_step, react_step, step_sum = block_pair(x_host, charges, x_seen, q_seen, False, True)
            return (force_run + force_step, energy_run + step_sum, x_seen, q_seen, react_run + react_step)

        force_acc, energy_acc, x_vis, q_vis, react_acc = lax.fori_loop(1, odd_steps, pair_step, (force_acc, energy_acc, x_vis, q_vis, react_acc))
    if blk_size % 2 == 0:
        x_vis = lax.ppermute(x_vis, "blk", next_perm)
        q_vis = lax.ppermute(q_vis, "blk", next_perm)
        if odd_steps >= 1:
            react_acc = lax.ppermute(react_acc, "blk", next_perm)
        mid_row = host_rows // 2
        is_lower = my_index < half_way
        x_a = jnp.where(is_lower, x_host[:mid_row], x_vis[mid_row:])
        q_a = jnp.where(is_lower, charges[:mid_row], q_vis[mid_row:])
        x_b = jnp.where(is_lower, x_vis, x_host)
        q_b = jnp.where(is_lower, q_vis, charges)
        force_half, react_full, pair_sum = block_pair(x_a, q_a, x_b, q_b, False, True)
        zero_half = jnp.zeros((mid_row, feat_dim), jnp.float32)
        force_acc = force_acc + jnp.where(is_lower, jnp.concatenate([force_half, zero_half]), react_full)
        react_acc = react_acc + jnp.where(is_lower, react_full, jnp.concatenate([zero_half, force_half]))
        energy_acc = energy_acc + pair_sum
    react_home = lax.ppermute(react_acc, "blk", home_perm)
    return (force_acc + react_home) / feat_dim, energy_acc


def solution(mesh):
    blk_size = mesh.shape["blk"]
    row_spec = P(("sys", "blk"), None)
    vec_spec = P(("sys", "blk"))

    def local_steps(positions, velocity, charges):
        force_zero, _ = paired_forces(positions, charges, blk_size)
        pos_one = positions + STEP_SIZE * velocity
        vel_one = velocity + STEP_SIZE * force_zero
        force_one, energy_local = paired_forces(pos_one, charges, blk_size)
        energy_one = lax.psum(energy_local, "blk").reshape(1)
        return force_one, energy_one, pos_one + STEP_SIZE * vel_one, vel_one + STEP_SIZE * force_one

    return jax.shard_map(local_steps, mesh=mesh, in_specs=(row_spec, row_spec, vec_spec), out_specs=(row_spec, P("sys"), row_spec, row_spec), check_vma=False)
```

profile of v0, /device:TPU:21, one launch (start us, length us, event | category | flops | bytes accessed | tf_op | source)
XLA Modules:
  0.0 835.5 jit_solution(18099476928941054304)
XLA Ops:
  0.6 3.1 multiply_reduce_fusion.3
  3.7 3.2 collective-permute-start.7
  9.2 26.1 %while.160 = (s32[]{:T(128)}, f32[]{:T(128)}, f32[4,256,256]{2,1,0:T(8,128)S(1)}, s32[4]{0:T(128)S(1)}, f32[1024]{0:T(1024)}, /*index=5*/f32[1024]{0:T(1024)S(1)...) while((s32[]{:T(128)}, f32[]{:T(128)}, ...), condition=%wide.region_4.5_spmd.clone, body=%wide.region_1.4_spmd.clone.sunk | while | flops 272039936 | bytes 2640587 | solution.py:43
  11.3 2.4 fusion.229
  24.3 2.4 fusion.229
  30.9 2.4 fusion.229
  36.3 21.0 %while.161 = (s32[]{:T(128)}, f32[4,256,256]{2,1,0:T(8,128)S(1)}, s32[4]{0:T(128)S(1)}, f32[1024]{0:T(1024)}, f32[1024]{0:T(1024)S(1)}, /*index=5*/bf16[1024,256...) while((s32[]{:T(128)}, f32[4,256,256]{2,1,0:T(8,128)S(1)}, s32[4]{0:T(128)S(1)}, ...), condition=%wide.region_31.32_spmd.clone, body=%wide.region_29.31_spmd.clone.sunk | while | flops 271777792 | bytes 2640563 | solution.py:43
  59.7 32.1 %while.162 = (s32[]{:T(128)}, f32[1024]{0:T(1024)S(1)}, f32[1024,256]{1,0:T(8,128)S(1)}, f32[]{:T(128)}, f32[4,256,256]{2,1,0:T(8,128)S(1)}, /*index=5*/s32[4]{0...) while((s32[]{:T(128)}, f32[1024]{0:T(1024)S(1)}, ...), condition=%wide.region_10.11_spmd.clone, body=%wide.region_6.0_spmd.clone.sunk | while | flops 406520576 | bytes 5406978 | solution.py:43
  61.8 2.5 fusion.241
  69.8 2.5 fusion.241
  77.8 2.5 fusion.241
  85.8 2.5 fusion.241
  95.4 285.6 %while.157 = (s32[]{:T(128)}, f32[1024,256]{1,0:T(8,128)S(1)}, f32[]{:T(128)}, bf16[1024,256]{1,0:T(8,128)(2,1)}, f32[1024]{0:T(1024)S(1)}, /*index=5*/f32[1024,...) while((s32[]{:T(128)}, f32[1024,256]{1,0:T(8,128)S(1)}, ...), condition=%wide.region_19.20_spmd, body=%wide.region_11.19_spmd.sunk | while | flops 409402112 | bytes 20649136 | solution.py:78
  98.9 2.6 collective-permute-done.3
  101.7 34.2 %while.166 = (s32[]{:T(128)}, f32[1024]{0:T(1024)S(1)}, f32[1024,256]{1,0:T(8,128)S(1)}, f32[]{:T(128)}, f32[4,256,256]{2,1,0:T(8,128)}, /*index=5*/s32[4]{0:T(1...) while((s32[]{:T(128)}, f32[1024]{0:T(1024)S(1)}, ...), condition=%wide.region_18.18_spmd.clone, body=%wide.region_14.17_spmd.clone.sunk | while | flops 406520576 | bytes 5407486 | solution.py:43
  138.3 2.4 fusion.223
  140.7 2.5 collective-permute-start.4
  146.7 2.6 collective-permute-done.3
  149.6 34.2 %while.166 = (s32[]{:T(128)}, f32[1024]{0:T(1024)S(1)}, f32[1024,256]{1,0:T(8,128)S(1)}, f32[]{:T(128)}, f32[4,256,256]{2,1,0:T(8,128)}, /*index=5*/s32[4]{0:T(1...) while((s32[]{:T(128)}, f32[1024]{0:T(1024)S(1)}, ...), condition=%wide.region_18.18_spmd.clone, body=%wide.region_14.17_spmd.clone.sunk | while | flops 406520576 | bytes 5407486 | solution.py:43
  186.1 2.4 fusion.223
  188.5 2.5 collective-permute-start.4
  194.5 2.6 collective-permute-done.3
  197.4 34.2 %while.166 = (s32[]{:T(128)}, f32[1024]{0:T(1024)S(1)}, f32[1024,256]{1,0:T(8,128)S(1)}, f32[]{:T(128)}, f32[4,256,256]{2,1,0:T(8,128)}, /*index=5*/s32[4]{0:T(1...) while((s32[]{:T(128)}, f32[1024]{0:T(1024)S(1)}, ...), condition=%wide.region_18.18_spmd.clone, body=%wide.region_14.17_spmd.clone.sunk | while | flops 406520576 | bytes 5407486 | solution.py:43
  233.9 2.4 fusion.223
  236.3 2.5 collective-permute-start.4
  242.3 2.6 collective-permute-done.3
  245.2 34.2 %while.166 = (s32[]{:T(128)}, f32[1024]{0:T(1024)S(1)}, f32[1024,256]{1,0:T(8,128)S(1)}, f32[]{:T(128)}, f32[4,256,256]{2,1,0:T(8,128)}, /*index=5*/s32[4]{0:T(1...) while((s32[]{:T(128)}, f32[1024]{0:T(1024)S(1)}, ...), condition=%wide.region_18.18_spmd.clone, body=%wide.region_14.17_spmd.clone.sunk | while | flops 406520576 | bytes 5407486 | solution.py:43
  281.7 2.4 fusion.223
  284.1 2.5 collective-permute-start.4
  290.1 2.7 collective-permute-done.3
  293.0 34.2 %while.166 = (s32[]{:T(128)}, f32[1024]{0:T(1024)S(1)}, f32[1024,256]{1,0:T(8,128)S(1)}, f32[]{:T(128)}, f32[4,256,256]{2,1,0:T(8,128)}, /*index=5*/s32[4]{0:T(1...) while((s32[]{:T(128)}, f32[1024]{0:T(1024)S(1)}, ...), condition=%wide.region_18.18_spmd.clone, body=%wide.region_14.17_spmd.clone.sunk | while | flops 406520576 | bytes 5407486 | solution.py:43
  329.5 2.4 fusion.223
  332.0 2.4 collective-permute-start.4
  337.9 3.9 collective-permute-done.3
  342.1 34.2 %while.166 = (s32[]{:T(128)}, f32[1024]{0:T(1024)S(1)}, f32[1024,256]{1,0:T(8,128)S(1)}, f32[]{:T(128)}, f32[4,256,256]{2,1,0:T(8,128)}, /*index=5*/s32[4]{0:T(1...) while((s32[]{:T(128)}, f32[1024]{0:T(1024)S(1)}, ...), condition=%wide.region_18.18_spmd.clone, body=%wide.region_14.17_spmd.clone.sunk | while | flops 406520576 | bytes 5407486 | solution.py:43
  378.6 2.4 fusion.223
  384.6 29.4 %while.164 = (s32[]{:T(128)}, f32[1024]{0:T(1024)S(1)}, f32[1024,256]{1,0:T(8,128)S(1)}, f32[4,256,256]{2,1,0:T(8,128)}, s32[4]{0:T(128)S(1)}, /*index=5*/f32[10...) while((s32[]{:T(128)}, f32[1024]{0:T(1024)S(1)}, ...), condition=%wide.region_36.37_spmd.clone, body=%wide.region_33.36_spmd.clone.sunk | while | flops 406258432 | bytes 5407462 | solution.py:43
  419.0 258.1 %while.159 = (s32[]{:T(128)}, f32[1024,256]{1,0:T(8,128)S(1)}, bf16[1024,256]{1,0:T(8,128)(2,1)}, f32[1024]{0:T(1024)S(1)}, f32[1024,256]{1,0:T(8,128)}, /*index...) while((s32[]{:T(128)}, f32[1024,256]{1,0:T(8,128)S(1)}, ...), condition=%wide.region_44.45_spmd, body=%wide.region_37.44_spmd.sunk | while | flops 409139968 | bytes 20649068 | solution.py:78
  421.2 3.5 collective-permute-start
  428.4 28.4 %while.167 = (s32[]{:T(128)}, f32[1024]{0:T(1024)S(1)}, f32[1024,256]{1,0:T(8,128)S(1)}, f32[4,256,256]{2,1,0:T(8,128)}, s32[4]{0:T(128)S(1)}, /*index=5*/f32[10...) while((s32[]{:T(128)}, f32[1024]{0:T(1024)S(1)}, ...), condition=%wide.region_43.43_spmd.clone, body=%wide.region_40.42_spmd.clone.sunk | while | flops 406258432 | bytes 5407462 | solution.py:43
  461.4 2.7 collective-permute-start.1
  464.2 3.7 collective-permute-start
  471.5 28.4 %while.167 = (s32[]{:T(128)}, f32[1024]{0:T(1024)S(1)}, f32[1024,256]{1,0:T(8,128)S(1)}, f32[4,256,256]{2,1,0:T(8,128)}, s32[4]{0:T(128)S(1)}, /*index=5*/f32[10...) while((s32[]{:T(128)}, f32[1024]{0:T(1024)S(1)}, ...), condition=%wide.region_43.43_spmd.clone, body=%wide.region_40.42_spmd.clone.sunk | while | flops 406258432 | bytes 5407462 | solution.py:43
  504.6 2.7 collective-permute-start.1
  507.3 2.5 collective-permute-start
  511.1 3.3 collective-permute-done
  514.6 28.4 %while.167 = (s32[]{:T(128)}, f32[1024]{0:T(1024)S(1)}, f32[1024,256]{1,0:T(8,128)S(1)}, f32[4,256,256]{2,1,0:T(8,128)}, s32[4]{0:T(128)S(1)}, /*index=5*/f32[10...) while((s32[]{:T(128)}, f32[1024]{0:T(1024)S(1)}, ...), condition=%wide.region_43.43_spmd.clone, body=%wide.region_40.42_spmd.clone.sunk | while | flops 406258432 | bytes 5407462 | solution.py:43
  549.3 2.5 collective-permute-start
  553.1 4.5 collective-permute-done
  557.8 28.4 %while.167 = (s32[]{:T(128)}, f32[1024]{0:T(1024)S(1)}, f32[1024,256]{1,0:T(8,128)S(1)}, f32[4,256,256]{2,1,0:T(8,128)}, s32[4]{0:T(128)S(1)}, /*index=5*/f32[10...) while((s32[]{:T(128)}, f32[1024]{0:T(1024)S(1)}, ...), condition=%wide.region_43.43_spmd.clone, body=%wide.region_40.42_spmd.clone.sunk | while | flops 406258432 | bytes 5407462 | solution.py:43
  591.2 2.5 collective-permute-start
  595.4 5.3 collective-permute-done
  600.9 28.4 %while.167 = (s32[]{:T(128)}, f32[1024]{0:T(1024)S(1)}, f32[1024,256]{1,0:T(8,128)S(1)}, f32[4,256,256]{2,1,0:T(8,128)}, s32[4]{0:T(128)S(1)}, /*index=5*/f32[10...) while((s32[]{:T(128)}, f32[1024]{0:T(1024)S(1)}, ...), condition=%wide.region_43.43_spmd.clone, body=%wide.region_40.42_spmd.clone.sunk | while | flops 406258432 | bytes 5407462 | solution.py:43
  638.6 5.3 collective-permute-done
  644.1 28.4 %while.167 = (s32[]{:T(128)}, f32[1024]{0:T(1024)S(1)}, f32[1024,256]{1,0:T(8,128)S(1)}, f32[4,256,256]{2,1,0:T(8,128)}, s32[4]{0:T(128)S(1)}, /*index=5*/f32[10...) while((s32[]{:T(128)}, f32[1024]{0:T(1024)S(1)}, ...), condition=%wide.region_43.43_spmd.clone, body=%wide.region_40.42_spmd.clone.sunk | while | flops 406258432 | bytes 5407462 | solution.py:43
  677.6 2.8 collective-permute-start.14
  680.4 3.7 collective-permute-start.15
  692.1 9.3 %while.163 = (s32[]{:T(128)}, f32[1024]{0:T(1024)S(1)}, f32[1024,256]{1,0:T(8,128)S(1)}, f32[]{:T(128)}, f32[2,256,256]{2,1,0:T(8,128)}, /*index=5*/s32[2]{0:T(1...) while((s32[]{:T(128)}, f32[1024]{0:T(1024)S(1)}, ...), condition=%wide.region_26.27_spmd.clone, body=%wide.region_22.26_spmd.clone.sunk | while | flops 406520576 | bytes 5407486 | solution.py:43
  705.5 9.3 %while.165 = (s32[]{:T(128)}, f32[1024]{0:T(1024)S(1)}, f32[1024,256]{1,0:T(8,128)S(1)}, f32[2,256,256]{2,1,0:T(8,128)}, s32[2]{0:T(128)S(1)}, /*index=5*/f32[51...) while((s32[]{:T(128)}, f32[1024]{0:T(1024)S(1)}, ...), condition=%wide.region_50.51_spmd.clone, body=%wide.region_47.50_spmd.clone.sunk | while | flops 406258432 | bytes 7504642 | solution.py:43
  714.9 2.6 select_add_fusion.7
  717.5 5.1 collective-permute-start.11
  722.7 2.7 select_add_fusion.6
  725.6 103.8 %psum.7 = f32[1]{0:T(128)} all-reduce(f32[1]{0:T(128)} %bitcast.4), channel_id=1, replica_groups=mesh['sys'=4,'blk'=16] {'blk'}, use_global_device_ids=true, to_apply=%region_27.28 | all-reduce | flops 1 | bytes 8 | tf_op jit(solution)/shard_map/psum | solution.py:109
  829.4 4.5 multiply_add_fusion
  (705 shorter events, 531.3 us)
Async XLA Ops:
  3.7 54.6 %collective-permute-start.7 = (bf16[1024,256]{1,0:T(8,128)(2,1)}, bf16[1024,256]{1,0:T(8,128)(2,1)}, u32[]{:S(2)}, u32[]{:S(2)}) collective-permute-start(bf16[1024,256]{1,0:T(8,128)(2,1)} %get-tuple-element.2135), channel_id=1, source_target_pairs={{0,1},{1,2},{2,3},{3,4},{4,5},{5,6},{6,7},{7,8},{8,9},{9,10},{10,1... | collective-permute-start | bytes 1572872 | tf_op jit(solution)/shard_map/ppermute | solution.py:64
  6.9 51.4 %collective-permute-start.6 = (f32[1024]{0:T(1024)}, f32[1024]{0:T(1024)S(1)}, u32[]{:S(2)}, u32[]{:S(2)}) collective-permute-start(f32[1024]{0:T(1024)} %param.25), channel_id=1, source_target_pairs={{0,1},{1,2},{2,3},{3,4},{4,5},{5,6},{6,7},{7,8},{8,9},{9,10},{10,1... | collective-permute-start | bytes 12296 | tf_op jit(solution)/shard_map/ppermute | solution.py:65
  6.9 375.4 %collective-permute-start.12 = (bf16[1024,256]{1,0:T(8,128)(2,1)}, bf16[1024,256]{1,0:T(8,128)(2,1)}, u32[]{:S(2)}, u32[]{:S(2)}) collective-permute-start(bf16[1024,256]{1,0:T(8,128)(2,1)} %get-tuple-element.2014), channel_id=1, source_target_pairs={{0,1},{1,2},{2,3},{3,4},{4,5},{5,6},{6,7},{7,8},{8,9},{9,10},{10,1... | collective-permute-start | bytes 1572872 | tf_op jit(solution)/shard_map/ppermute | solution.py:64
  35.3 1.0 copy-start.10
  57.3 1.0 copy-start.11
  95.4 6.2 collective-permute-start.4
  95.4 6.1 collective-permute-start.3
  97.6 40.6 %collective-permute-start.5 = (f32[1024,256]{1,0:T(8,128)}, f32[1024,256]{1,0:T(8,128)}, u32[]{:S(2)}, u32[]{:S(2)}) collective-permute-start(f32[1024,256]{1,0:T(8,128)} %get-tuple-element.2149), channel_id=1, source_target_pairs={{0,1},{1,2},{2,3},{3,4},{4,5},{5,6},{6,7},{7,8},{8,9},{9,10},{10,1... | collective-permute-start | bytes 3145736 | tf_op jit(solution)/shard_map/while/body/eval_jaxpr/ppermute | solution.py:74
  140.7 8.7 %collective-permute-start.4 = (bf16[1024,256]{1,0:T(8,128)(2,1)}, bf16[1024,256]{1,0:T(8,128)(2,1)S(1)}, u32[]{:S(2)}, u32[]{:S(2)}) collective-permute-start(bf16[1024,256]{1,0:T(8,128)(2,1)} %get-tuple-element.2147), channel_id=1, source_target_pairs={{0,1},{1,2},{2,3},{3,4},{4,5},{5,6},{6,7},{7,8},{8,9},{9,10},{10,1... | collective-permute-start | bytes 1572872 | tf_op jit(solution)/shard_map/while/body/eval_jaxpr/ppermute | solution.py:72
  143.2 6.1 collective-permute-start.3
  143.2 42.9 %collective-permute-start.5 = (f32[1024,256]{1,0:T(8,128)}, f32[1024,256]{1,0:T(8,128)}, u32[]{:S(2)}, u32[]{:S(2)}) collective-permute-start(f32[1024,256]{1,0:T(8,128)} %get-tuple-element.2149), channel_id=1, source_target_pairs={{0,1},{1,2},{2,3},{3,4},{4,5},{5,6},{6,7},{7,8},{8,9},{9,10},{10,1... | collective-permute-start | bytes 3145736 | tf_op jit(solution)/shard_map/while/body/eval_jaxpr/ppermute | solution.py:74
  188.5 8.7 %collective-permute-start.4 = (bf16[1024,256]{1,0:T(8,128)(2,1)}, bf16[1024,256]{1,0:T(8,128)(2,1)S(1)}, u32[]{:S(2)}, u32[]{:S(2)}) collective-permute-start(bf16[1024,256]{1,0:T(8,128)(2,1)} %get-tuple-element.2147), channel_id=1, source_target_pairs={{0,1},{1,2},{2,3},{3,4},{4,5},{5,6},{6,7},{7,8},{8,9},{9,10},{10,1... | collective-permute-start | bytes 1572872 | tf_op jit(solution)/shard_map/while/body/eval_jaxpr/ppermute | solution.py:72
  191.0 6.1 collective-permute-start.3
  191.0 42.9 %collective-permute-start.5 = (f32[1024,256]{1,0:T(8,128)}, f32[1024,256]{1,0:T(8,128)}, u32[]{:S(2)}, u32[]{:S(2)}) collective-permute-start(f32[1024,256]{1,0:T(8,128)} %get-tuple-element.2149), channel_id=1, source_target_pairs={{0,1},{1,2},{2,3},{3,4},{4,5},{5,6},{6,7},{7,8},{8,9},{9,10},{10,1... | collective-permute-start | bytes 3145736 | tf_op jit(solution)/shard_map/while/body/eval_jaxpr/ppermute | solution.py:74
  236.3 8.7 %collective-permute-start.4 = (bf16[1024,256]{1,0:T(8,128)(2,1)}, bf16[1024,256]{1,0:T(8,128)(2,1)S(1)}, u32[]{:S(2)}, u32[]{:S(2)}) collective-permute-start(bf16[1024,256]{1,0:T(8,128)(2,1)} %get-tuple-element.2147), channel_id=1, source_target_pairs={{0,1},{1,2},{2,3},{3,4},{4,5},{5,6},{6,7},{7,8},{8,9},{9,10},{10,1... | collective-permute-start | bytes 1572872 | tf_op jit(solution)/shard_map/while/body/eval_jaxpr/ppermute | solution.py:72
  238.8 6.1 collective-permute-start.3
  238.8 42.9 %collective-permute-start.5 = (f32[1024,256]{1,0:T(8,128)}, f32[1024,256]{1,0:T(8,128)}, u32[]{:S(2)}, u32[]{:S(2)}) collective-permute-start(f32[1024,256]{1,0:T(8,128)} %get-tuple-element.2149), channel_id=1, source_target_pairs={{0,1},{1,2},{2,3},{3,4},{4,5},{5,6},{6,7},{7,8},{8,9},{9,10},{10,1... | collective-permute-start | bytes 3145736 | tf_op jit(solution)/shard_map/while/body/eval_jaxpr/ppermute | solution.py:74
  284.1 8.7 %collective-permute-start.4 = (bf16[1024,256]{1,0:T(8,128)(2,1)}, bf16[1024,256]{1,0:T(8,128)(2,1)S(1)}, u32[]{:S(2)}, u32[]{:S(2)}) collective-permute-start(bf16[1024,256]{1,0:T(8,128)(2,1)} %get-tuple-element.2147), channel_id=1, source_target_pairs={{0,1},{1,2},{2,3},{3,4},{4,5},{5,6},{6,7},{7,8},{8,9},{9,10},{10,1... | collective-permute-start | bytes 1572872 | tf_op jit(solution)/shard_map/while/body/eval_jaxpr/ppermute | solution.py:72
  286.6 6.2 collective-permute-start.3
  286.6 42.9 %collective-permute-start.5 = (f32[1024,256]{1,0:T(8,128)}, f32[1024,256]{1,0:T(8,128)}, u32[]{:S(2)}, u32[]{:S(2)}) collective-permute-start(f32[1024,256]{1,0:T(8,128)} %get-tuple-element.2149), channel_id=1, source_target_pairs={{0,1},{1,2},{2,3},{3,4},{4,5},{5,6},{6,7},{7,8},{8,9},{9,10},{10,1... | collective-permute-start | bytes 3145736 | tf_op jit(solution)/shard_map/while/body/eval_jaxpr/ppermute | solution.py:74
  332.0 9.9 %collective-permute-start.4 = (bf16[1024,256]{1,0:T(8,128)(2,1)}, bf16[1024,256]{1,0:T(8,128)(2,1)S(1)}, u32[]{:S(2)}, u32[]{:S(2)}) collective-permute-start(bf16[1024,256]{1,0:T(8,128)(2,1)} %get-tuple-element.2147), channel_id=1, source_target_pairs={{0,1},{1,2},{2,3},{3,4},{4,5},{5,6},{6,7},{7,8},{8,9},{9,10},{10,1... | collective-permute-start | bytes 1572872 | tf_op jit(solution)/shard_map/while/body/eval_jaxpr/ppermute | solution.py:72
  334.4 7.4 collective-permute-start.3
  334.4 44.1 %collective-permute-start.5 = (f32[1024,256]{1,0:T(8,128)}, f32[1024,256]{1,0:T(8,128)}, u32[]{:S(2)}, u32[]{:S(2)}) collective-permute-start(f32[1024,256]{1,0:T(8,128)} %get-tuple-element.2149), channel_id=1, source_target_pairs={{0,1},{1,2},{2,3},{3,4},{4,5},{5,6},{6,7},{7,8},{8,9},{9,10},{10,1... | collective-permute-start | bytes 3145736 | tf_op jit(solution)/shard_map/while/body/eval_jaxpr/ppermute | solution.py:74
  381.0 3.6 copy-start
  381.0 3.6 copy-start.3
  381.0 306.7 %collective-permute-start.9 = (bf16[1024,256]{1,0:T(8,128)(2,1)}, bf16[1024,256]{1,0:T(8,128)(2,1)}, u32[]{:S(2)}, u32[]{:S(2)}) collective-permute-start(bf16[1024,256]{1,0:T(8,128)(2,1)} %get-tuple-element.592), channel_id=1, source_target_pairs={{0,1},{1,2},{2,3},{3,4},{4,5},{5,6},{6,7},{7,8},{8,9},{9,10},{10,1... | collective-permute-start | bytes 1572872 | tf_op jit(solution)/shard_map/ppermute | solution.py:80
  382.2 298.2 %collective-permute-start.8 = (f32[1024]{0:T(1024)S(1)}, f32[1024]{0:T(1024)S(1)}, u32[]{:S(2)}, u32[]{:S(2)}) collective-permute-start(f32[1024]{0:T(1024)S(1)} %get-tuple-element.591), channel_id=1, source_target_pairs={{0,1},{1,2},{2,3},{3,4},{4,5},{5,6},{6,7},{7,8},{8,9},{9,10},{10,1... | collective-permute-start | bytes 12296 | tf_op jit(solution)/shard_map/ppermute | solution.py:81
  414.0 1.0 copy-start.4
  414.9 1.9 copy-start.5
  419.0 9.1 %collective-permute-start.1 = (bf16[1024,256]{1,0:T(8,128)(2,1)}, bf16[1024,256]{1,0:T(8,128)(2,1)S(1)}, u32[]{:S(2)}, u32[]{:S(2)}) collective-permute-start(bf16[1024,256]{1,0:T(8,128)(2,1)} %get-tuple-element.2024), channel_id=1, source_target_pairs={{0,1},{1,2},{2,3},{3,4},{4,5},{5,6},{6,7},{7,8},{8,9},{9,10},{10,1... | collective-permute-start | bytes 1572872 | tf_op jit(solution)/shard_map/while/body/eval_jaxpr/ppermute | solution.py:72
  421.2 6.9 collective-permute-start
  424.7 34.3 %collective-permute-start.2 = (f32[1024,256]{1,0:T(8,128)}, f32[1024,256]{1,0:T(8,128)}, u32[]{:S(2)}, u32[]{:S(2)}) collective-permute-start(f32[1024,256]{1,0:T(8,128)} %get-tuple-element.2026), channel_id=1, source_target_pairs={{0,1},{1,2},{2,3},{3,4},{4,5},{5,6},{6,7},{7,8},{8,9},{9,10},{10,1... | collective-permute-start | bytes 3145736 | tf_op jit(solution)/shard_map/while/body/eval_jaxpr/ppermute | solution.py:74
  461.4 9.9 %collective-permute-start.1 = (bf16[1024,256]{1,0:T(8,128)(2,1)}, bf16[1024,256]{1,0:T(8,128)(2,1)S(1)}, u32[]{:S(2)}, u32[]{:S(2)}) collective-permute-start(bf16[1024,256]{1,0:T(8,128)(2,1)} %get-tuple-element.2024), channel_id=1, source_target_pairs={{0,1},{1,2},{2,3},{3,4},{4,5},{5,6},{6,7},{7,8},{8,9},{9,10},{10,1... | collective-permute-start | bytes 1572872 | tf_op jit(solution)/shard_map/while/body/eval_jaxpr/ppermute | solution.py:72
  464.2 7.1 collective-permute-start
  467.9 34.3 %collective-permute-start.2 = (f32[1024,256]{1,0:T(8,128)}, f32[1024,256]{1,0:T(8,128)}, u32[]{:S(2)}, u32[]{:S(2)}) collective-permute-start(f32[1024,256]{1,0:T(8,128)} %get-tuple-element.2026), channel_id=1, source_target_pairs={{0,1},{1,2},{2,3},{3,4},{4,5},{5,6},{6,7},{7,8},{8,9},{9,10},{10,1... | collective-permute-start | bytes 3145736 | tf_op jit(solution)/shard_map/while/body/eval_jaxpr/ppermute | solution.py:74
  504.6 9.8 %collective-permute-start.1 = (bf16[1024,256]{1,0:T(8,128)(2,1)}, bf16[1024,256]{1,0:T(8,128)(2,1)S(1)}, u32[]{:S(2)}, u32[]{:S(2)}) collective-permute-start(bf16[1024,256]{1,0:T(8,128)(2,1)} %get-tuple-element.2024), channel_id=1, source_target_pairs={{0,1},{1,2},{2,3},{3,4},{4,5},{5,6},{6,7},{7,8},{8,9},{9,10},{10,1... | collective-permute-start | bytes 1572872 | tf_op jit(solution)/shard_map/while/body/eval_jaxpr/ppermute | solution.py:72
  507.3 7.1 collective-permute-start
  509.8 35.5 %collective-permute-start.2 = (f32[1024,256]{1,0:T(8,128)}, f32[1024,256]{1,0:T(8,128)}, u32[]{:S(2)}, u32[]{:S(2)}) collective-permute-start(f32[1024,256]{1,0:T(8,128)} %get-tuple-element.2026), channel_id=1, source_target_pairs={{0,1},{1,2},{2,3},{3,4},{4,5},{5,6},{6,7},{7,8},{8,9},{9,10},{10,1... | collective-permute-start | bytes 3145736 | tf_op jit(solution)/shard_map/while/body/eval_jaxpr/ppermute | solution.py:74
  547.7 9.9 %collective-permute-start.1 = (bf16[1024,256]{1,0:T(8,128)(2,1)}, bf16[1024,256]{1,0:T(8,128)(2,1)S(1)}, u32[]{:S(2)}, u32[]{:S(2)}) collective-permute-start(bf16[1024,256]{1,0:T(8,128)(2,1)} %get-tuple-element.2024), channel_id=1, source_target_pairs={{0,1},{1,2},{2,3},{3,4},{4,5},{5,6},{6,7},{7,8},{8,9},{9,10},{10,1... | collective-permute-start | bytes 1572872 | tf_op jit(solution)/shard_map/while/body/eval_jaxpr/ppermute | solution.py:72
  549.3 8.3 collective-permute-start
  551.8 36.7 %collective-permute-start.2 = (f32[1024,256]{1,0:T(8,128)}, f32[1024,256]{1,0:T(8,128)}, u32[]{:S(2)}, u32[]{:S(2)}) collective-permute-start(f32[1024,256]{1,0:T(8,128)} %get-tuple-element.2026), channel_id=1, source_target_pairs={{0,1},{1,2},{2,3},{3,4},{4,5},{5,6},{6,7},{7,8},{8,9},{9,10},{10,1... | collective-permute-start | bytes 3145736 | tf_op jit(solution)/shard_map/while/body/eval_jaxpr/ppermute | solution.py:74
  590.9 9.9 %collective-permute-start.1 = (bf16[1024,256]{1,0:T(8,128)(2,1)}, bf16[1024,256]{1,0:T(8,128)(2,1)S(1)}, u32[]{:S(2)}, u32[]{:S(2)}) collective-permute-start(bf16[1024,256]{1,0:T(8,128)(2,1)} %get-tuple-element.2024), channel_id=1, source_target_pairs={{0,1},{1,2},{2,3},{3,4},{4,5},{5,6},{6,7},{7,8},{8,9},{9,10},{10,1... | collective-permute-start | bytes 1572872 | tf_op jit(solution)/shard_map/while/body/eval_jaxpr/ppermute | solution.py:72
  591.2 9.5 %collective-permute-start = (f32[1024]{0:T(1024)S(1)}, f32[1024]{0:T(1024)S(1)}, u32[]{:S(2)}, u32[]{:S(2)}) collective-permute-start(f32[1024]{0:T(1024)S(1)} %get-tuple-element.2025), channel_id=1, source_target_pairs={{0,1},{1,2},{2,3},{3,4},{4,5},{5,6},{6,7},{7,8},{8,9},{9,10},{10,1... | collective-permute-start | bytes 12296 | tf_op jit(solution)/shard_map/while/body/eval_jaxpr/ppermute | solution.py:73
  593.7 37.9 %collective-permute-start.2 = (f32[1024,256]{1,0:T(8,128)}, f32[1024,256]{1,0:T(8,128)}, u32[]{:S(2)}, u32[]{:S(2)}) collective-permute-start(f32[1024,256]{1,0:T(8,128)} %get-tuple-element.2026), channel_id=1, source_target_pairs={{0,1},{1,2},{2,3},{3,4},{4,5},{5,6},{6,7},{7,8},{8,9},{9,10},{10,1... | collective-permute-start | bytes 3145736 | tf_op jit(solution)/shard_map/while/body/eval_jaxpr/ppermute | solution.py:74
  634.0 9.9 %collective-permute-start.1 = (bf16[1024,256]{1,0:T(8,128)(2,1)}, bf16[1024,256]{1,0:T(8,128)(2,1)S(1)}, u32[]{:S(2)}, u32[]{:S(2)}) collective-permute-start(bf16[1024,256]{1,0:T(8,128)(2,1)} %get-tuple-element.2024), channel_id=1, source_target_pairs={{0,1},{1,2},{2,3},{3,4},{4,5},{5,6},{6,7},{7,8},{8,9},{9,10},{10,1... | collective-permute-start | bytes 1572872 | tf_op jit(solution)/shard_map/while/body/eval_jaxpr/ppermute | solution.py:72
  634.0 9.9 %collective-permute-start = (f32[1024]{0:T(1024)S(1)}, f32[1024]{0:T(1024)S(1)}, u32[]{:S(2)}, u32[]{:S(2)}) collective-permute-start(f32[1024]{0:T(1024)S(1)} %get-tuple-element.2025), channel_id=1, source_target_pairs={{0,1},{1,2},{2,3},{3,4},{4,5},{5,6},{6,7},{7,8},{8,9},{9,10},{10,1... | collective-permute-start | bytes 12296 | tf_op jit(solution)/shard_map/while/body/eval_jaxpr/ppermute | solution.py:73
  635.6 39.1 %collective-permute-start.2 = (f32[1024,256]{1,0:T(8,128)}, f32[1024,256]{1,0:T(8,128)}, u32[]{:S(2)}, u32[]{:S(2)}) collective-permute-start(f32[1024,256]{1,0:T(8,128)} %get-tuple-element.2026), channel_id=1, source_target_pairs={{0,1},{1,2},{2,3},{3,4},{4,5},{5,6},{6,7},{7,8},{8,9},{9,10},{10,1... | collective-permute-start | bytes 3145736 | tf_op jit(solution)/shard_map/while/body/eval_jaxpr/ppermute | solution.py:74
  677.2 13.7 %copy-start.2 = (f32[1024,256]{1,0:T(8,128)}, f32[1024,256]{1,0:T(8,128)S(1)}, u32[]{:S(2)}) copy-start(f32[1024,256]{1,0:T(8,128)S(1)} %get-tuple-element.603) | copy-start | bytes 3145732
  677.2 9.1 %collective-permute-start.13 = (f32[1024]{0:T(1024)S(1)}, f32[1024]{0:T(1024)S(1)}, u32[]{:S(2)}, u32[]{:S(2)}) collective-permute-start(f32[1024]{0:T(1024)S(1)} %get-tuple-element.604), channel_id=1, source_target_pairs={{0,1},{1,2},{2,3},{3,4},{4,5},{5,6},{6,7},{7,8},{8,9},{9,10},{10,1... | collective-permute-start | bytes 12296 | tf_op jit(solution)/shard_map/ppermute | solution.py:81
  677.2 37.7 %collective-permute-start.10 = (f32[1024,256]{1,0:T(8,128)}, f32[1024,256]{1,0:T(8,128)}, u32[]{:S(2)}, u32[]{:S(2)}) collective-permute-start(f32[1024,256]{1,0:T(8,128)} %get-tuple-element.596), channel_id=1, source_target_pairs={{0,1},{1,2},{2,3},{3,4},{4,5},{5,6},{6,7},{7,8},{8,9},{9,10},{10,1... | collective-permute-start | bytes 3145736 | tf_op jit(solution)/shard_map/ppermute | solution.py:83
  677.6 23.9 %collective-permute-start.14 = (bf16[1024,256]{1,0:T(8,128)(2,1)}, bf16[1024,256]{1,0:T(8,128)(2,1)}, u32[]{:S(2)}, u32[]{:S(2)}) collective-permute-start(bf16[1024,256]{1,0:T(8,128)(2,1)} %get-tuple-element.605), channel_id=1, source_target_pairs={{0,1},{1,2},{2,3},{3,4},{4,5},{5,6},{6,7},{7,8},{8,9},{9,10},{10,1... | collective-permute-start | bytes 1572872 | tf_op jit(solution)/shard_map/ppermute | solution.py:80
  680.4 42.3 %collective-permute-start.15 = (f32[1024,256]{1,0:T(8,128)}, f32[1024,256]{1,0:T(8,128)}, u32[]{:S(2)}, u32[]{:S(2)}) collective-permute-start(f32[1024,256]{1,0:T(8,128)} %get-tuple-element.609), channel_id=1, source_target_pairs={{0,1},{1,2},{2,3},{3,4},{4,5},{5,6},{6,7},{7,8},{8,9},{9,10},{10,1... | collective-permute-start | bytes 3145736 | tf_op jit(solution)/shard_map/ppermute | solution.py:83
  690.9 1.2 copy-start.6
  706.9 1.8 copy-start.7
  711.6 1.8 copy-start.7
  714.9 7.8 copy-start.8
  717.5 111.9 %collective-permute-start.11 = (f32[1024,256]{1,0:T(8,128)}, f32[1024,256]{1,0:T(8,128)}, u32[]{:S(2)}, u32[]{:S(2)}) collective-permute-start(f32[1024,256]{1,0:T(8,128)} %select_add_fusion.7), channel_id=1, source_target_pairs={{0,8},{1,9},{2,10},{3,11},{4,12},{5,13},{6,14},{7,15},{8,0},{9,1},... | collective-permute-start | bytes 3145736 | tf_op jit(solution)/shard_map/ppermute | solution.py:95
  722.7 106.7 %copy-start.1 = (f32[1024,256]{1,0:T(8,128)S(1)}, f32[1024,256]{1,0:T(8,128)}, u32[]{:S(2)}) copy-start(f32[1024,256]{1,0:T(8,128)} %copy-done) | copy-start | bytes 3145732
  725.4 104.0 %collective-permute-start.16 = (f32[1024,256]{1,0:T(8,128)}, f32[1024,256]{1,0:T(8,128)}, u32[]{:S(2)}, u32[]{:S(2)}) collective-permute-start(f32[1024,256]{1,0:T(8,128)} %select_add_fusion.6), channel_id=1, source_target_pairs={{0,8},{1,9},{2,10},{3,11},{4,12},{5,13},{6,14},{7,15},{8,0},{9,1},... | collective-permute-start | bytes 3145736 | tf_op jit(solution)/shard_map/ppermute | solution.py:95
  829.4 4.6 copy-start.9
  829.4 4.5 copy-start.12
where the time goes:
time: 844 us; the launch traced here: 836 us
  matrix products  333 us (39%)
  local copies, waits for them, and re-layouts  114 us (14%)
  blocking collectives  104 us (12%)
  other arithmetic  96.7 us (11%)
  starting transfers between devices  73.1 us (9%)
  loops' own time  72 us (9%)
  waiting for transfers between devices  41.7 us (5%)
    dot_general x68, matrix products, tile_step(): jnp.einsum('id,jd->ij', x_tile, x_b, preferred_element_type=jnp.float32)  134 us
    dot_general x68, matrix products, tile_step(): pull_sum = jnp.dot(w_low, x_b, preferred_element_type=jnp.float32)  121 us
    psum x1, blocking collectives, local_steps(): energy_one = lax.psum(energy_local, 'blk').reshape(1)  104 us
    dot_general x60, matrix products, tile_step(): jnp.einsum('ij,id->jd', w_low, x_tile, preferred_element_type=jnp.float32)  79 us
    another operation x18, loops' own time, block_pair(): lax.scan(tile_step, start_state, jnp.arange(rows_a // tile_rows))  71.2 us
    dynamic_slice x68, local copies, waits for them, and re-layouts, tile_step(): q_tile = lax.dynamic_slice_in_dim(q_a, row_start, tile_rows, 0)  48.9 us
    dynamic_slice x68, local copies, waits for them, and re-layouts, block_pair(): lax.scan(tile_step, start_state, jnp.arange(rows_a // tile_rows))  43.7 us
    ppermute x12, waiting for transfers between devices, pair_step(): q_seen = lax.ppermute(q_seen, 'blk', next_perm)  39.5 us
  transfers between devices with their start and end apart: 47, of which 13 were waited for; matrix products, arithmetic and copies ran while one was open for 64% of the time, Pallas kernels for 0%

commit v1 on v0

v1 whole, which is shorter than its diff:
```python
import functools

import jax
import jax.numpy as jnp
from jax import lax
from jax.experimental import pallas as pl
from jax.experimental.pallas import tpu as pltpu
from jax.sharding import PartitionSpec as P

MESH = pl.DeviceIdType.MESH
STEP_SIZE = 0.5
LOG2E = 1.4426950408889634
LANES = 128
F32 = jnp.float32
BF16 = jnp.bfloat16


def kernel(n, x0_ref, v0_ref, q_ref, f1_ref, x2_ref, v2_ref, e_ref,
           xg, xl, aux, sc, qc, acc, rho, ebuf,
           send_r, recv_r, send_l, recv_l, send_s, recv_s, own_send, own_recv,
           asend_r, arecv_r, asend_l, arecv_l, asend_s, arecv_s, esend, erecv):
    rows, dim = x0_ref.shape
    unit = rows // 2
    sub = rows // 4
    chunks = rows // LANES
    half_way = n // 4
    scale = LOG2E / (2.0 * dim)
    me = lax.axis_index("blk")
    right = lax.rem(me + 2, n)
    left = lax.rem(me + n - 2, n)
    sib = me + 1 - 2 * lax.rem(me, 2)

    def push(ref, send, recv, target):
        pltpu.make_async_remote_copy(src_ref=ref, dst_ref=ref, send_sem=send, recv_sem=recv,
                                     device_id={"blk": target}, device_id_type=MESH).start()

    def await_recv(ref, send, recv):
        pltpu.make_async_remote_copy(src_ref=ref, dst_ref=ref, send_sem=send, recv_sem=recv,
                                     device_id={"blk": sib}, device_id_type=MESH).wait_recv()

    def await_send(ref, send, recv):
        pltpu.make_async_remote_copy(src_ref=ref, dst_ref=ref, send_sem=send, recv_sem=recv,
                                     device_id={"blk": sib}, device_id_type=MESH).wait_send()

    def unit_ref(ev, src, half):
        return xg.at[ev, src, pl.ds(pl.multiple_of(half * unit, unit), unit), :]

    barrier = pltpu.get_barrier_semaphore()

    @pl.loop(1, n)
    def _(p):
        pl.semaphore_signal(barrier, inc=1, device_id={"blk": lax.rem(me + p, n)}, device_id_type=MESH)

    aux[me, 0] = q_ref[...]

    @pl.loop(0, chunks)
    def _(c):
        rs = pl.ds(pl.multiple_of(c * LANES, LANES), LANES)
        pos = x0_ref[rs, :]
        for ev in (0, 1):
            if ev == 1:
                pos = pos + STEP_SIZE * v0_ref[rs, :]
            low = pos.astype(BF16)
            xg[ev, me, rs, :] = low
            wide = low.astype(F32)
            xl[ev, rs, :] = (wide * 2.0).astype(BF16)
            norm = jnp.broadcast_to(jnp.sum(wide * wide, axis=1, keepdims=True), (LANES, LANES))
            sc[ev, rs, :] = norm
            aux[me, 1 + ev, pl.ds(c, 1), :] = norm.T[0:1, :]
        qc[rs, :] = jnp.broadcast_to(q_ref[pl.ds(c, 1), :], (LANES, LANES)).T

    acc[...] = jnp.zeros_like(acc)
    rho[...] = jnp.zeros_like(rho)
    pl.semaphore_wait(barrier, n - 1)

    push(aux.at[me], asend_r.at[1], arecv_r.at[1], right)
    push(aux.at[me], asend_l.at[1], arecv_l.at[1], left)
    push(aux.at[me], asend_s.at[0, 0], arecv_s.at[0, 0], sib)
    for v in (1, 2, 3, 4):
        ev, hr = 1 - (v - 1) // 2, (v - 1) % 2
        push(unit_ref(ev, me, hr), send_r.at[v], recv_r.at[v], right)
        push(unit_ref(ev, me, 1 - hr), send_l.at[v], recv_l.at[v], left)
        if v % 2 == 1:
            push(xg.at[ev, me], own_send.at[ev], own_recv.at[ev], sib)

    def pair_unit(ev, src, half, own):
        xj = xg[ev, src, pl.ds(pl.multiple_of(half * unit, unit), unit), :]
        base = half * (unit // LANES)
        if own:
            diff = lax.broadcasted_iota(jnp.int32, (sub, LANES), 0) - lax.broadcasted_iota(jnp.int32, (sub, LANES), 1)
        for r in range(rows // sub):
            rs = pl.ds(r * sub, sub)
            gram = lax.dot_general(xl[ev, rs, :], xj, (((1,), (1,)), ((), ())), preferred_element_type=F32)
            norm_i = sc[ev, rs, :]
            q_i = qc[rs, :]
            low, total = [], None
            for c in range(unit // LANES):
                norm_j = aux[src, 1 + ev, pl.ds(base + c, 1), :]
                q_j = aux[src, 0, pl.ds(base + c, 1), :]
                neg = jnp.minimum(gram[:, c * LANES:(c + 1) * LANES] - (norm_i + norm_j), 0.0)
                weight = (q_i * q_j) * jnp.exp2(neg * scale)
                if own:
                    weight = jnp.where(diff == half * unit + (c * LANES - r * sub), 0.0, weight)
                total = weight if total is None else total + weight
                low.append(weight.astype(BF16))
            rho[ev, rs, :] += total
            acc[ev, rs, :] += jnp.dot(jnp.concatenate(low, axis=1), xj, preferred_element_type=F32)

    def pair_two(ev, src_a, half_a, src_b, half_b):
        @pl.loop(0, 2)
        def _(j):
            pair_unit(ev, src_a + j * (src_b - src_a), half_a + j * (half_b - half_a), False)

    @pl.loop(0, 4)
    def _(j):
        pair_unit(1 - j // 2, me, lax.rem(j, 2), True)

    await_recv(aux.at[sib], asend_s.at[0, 0], arecv_s.at[0, 0])

    @pl.loop(0, 2)
    def _(j):
        await_recv(xg.at[1 - j, sib], own_send.at[1 - j], own_recv.at[1 - j])
        pair_two(1 - j, sib, 0, sib, 1)

    last = 3 * half_way + 2

    @pl.loop(1, last + 1)
    def _(i):
        v = i + i // last
        hop = 1 + (v - 1) // 4
        m = lax.rem(v - 1, 4)
        ev = 1 - m // 2
        hr = lax.rem(m, 2)
        hl = 1 - hr
        src_r = lax.rem(me + n - 2 * hop, n)
        src_l = lax.rem(me + 2 * hop, n)
        sib_r = lax.rem(sib + n - 2 * hop, n)
        sib_l = lax.rem(sib + 2 * hop, n)
        onward = (hop < half_way - 1) | ((hop < half_way) & (hr == 0))

        @pl.when(m == 0)
        def _():
            await_recv(aux.at[src_r], asend_r.at[hop], arecv_r.at[hop])
            push(aux.at[src_r], asend_s.at[0, hop], arecv_s.at[0, hop], sib)

            @pl.when(hop < half_way)
            def _():
                push(aux.at[src_r], asend_r.at[hop + 1], arecv_r.at[hop + 1], right)
                await_recv(aux.at[src_l], asend_l.at[hop], arecv_l.at[hop])
                push(aux.at[src_l], asend_s.at[1, hop], arecv_s.at[1, hop], sib)

                @pl.when(hop < half_way - 1)
                def _():
                    push(aux.at[src_l], asend_l.at[hop + 1], arecv_l.at[hop + 1], left)

        await_recv(unit_ref(ev, src_r, hr), send_r.at[v], recv_r.at[v])

        @pl.when(onward)
        def _():
            push(unit_ref(ev, src_r, hr), send_r.at[v + 4], recv_r.at[v + 4], right)

        push(unit_ref(ev, src_r, hr), send_s.at[0, v], recv_s.at[0, v], sib)
        await_recv(unit_ref(ev, src_l, hl), send_l.at[v], recv_l.at[v])

        @pl.when(onward)
        def _():
            push(unit_ref(ev, src_l, hl), send_l.at[v + 4], recv_l.at[v + 4], left)

        push(unit_ref(ev, src_l, hl), send_s.at[1, v], recv_s.at[1, v], sib)

        @pl.when(i == last)
        def _():
            @pl.loop(1, n)
            def _(p):
                peer = lax.rem(me + p, n)
                push(ebuf.at[me], esend.at[peer], erecv.at[me], peer)

        pair_two(ev, src_r, hr, src_l, hl)

        @pl.when(m == 0)
        def _():
            await_recv(aux.at[sib_r], asend_s.at[0, hop], arecv_s.at[0, hop])

            @pl.when(hop < half_way)
            def _():
                await_recv(aux.at[sib_l], asend_s.at[1, hop], arecv_s.at[1, hop])

        await_recv(unit_ref(ev, sib_r, hr), send_s.at[0, v], recv_s.at[0, v])
        await_recv(unit_ref(ev, sib_l, hl), send_s.at[1, v], recv_s.at[1, v])
        pair_two(ev, sib_r, hr, sib_l, hl)

        @pl.when(i == last - 1)
        def _():
            ebuf[me] = jnp.broadcast_to(0.5 * jnp.sum(rho[1], keepdims=True), ebuf.shape[1:])

    @pl.loop(0, chunks)
    def _(c):
        rs = pl.ds(pl.multiple_of(c * LANES, LANES), LANES)
        force = [(jnp.sum(rho[ev, rs, :], axis=1, keepdims=True) * xg[ev, me, rs, :].astype(F32) - acc[ev, rs, :])
                 / dim for ev in (0, 1)]
        vel_zero = v0_ref[rs, :]
        vel_one = vel_zero + STEP_SIZE * force[0]
        f1_ref[rs, :] = force[1]
        x2_ref[rs, :] = (x0_ref[rs, :] + STEP_SIZE * vel_zero) + STEP_SIZE * vel_one
        v2_ref[rs, :] = vel_one + STEP_SIZE * force[1]

    @pl.loop(1, n)
    def _(p):
        peer = lax.rem(me + p, n)
        await_recv(ebuf.at[peer], esend.at[peer], erecv.at[peer])
        await_send(ebuf.at[me], esend.at[peer], erecv.at[me])

    e_ref[0] = jnp.sum(jnp.sum(ebuf[...], axis=0)[0:1, 0:1])

    @pl.loop(1, last + 1)
    def _(i):
        v = i + i // last
        piece = unit_ref(0, me, 0)
        await_send(piece, send_r.at[v], recv_r.at[v])
        await_send(piece, send_l.at[v], recv_l.at[v])
        await_send(piece, send_s.at[0, v], recv_s.at[0, v])
        await_send(piece, send_s.at[1, v], recv_s.at[1, v])

    for ev in (0, 1):
        await_send(xg.at[ev, me], own_send.at[ev], own_recv.at[ev])
    table = aux.at[me]
    await_send(table, asend_s.at[0, 0], arecv_s.at[0, 0])
    for hop in range(1, half_way + 1):
        await_send(table, asend_r.at[hop], arecv_r.at[hop])
        await_send(table, asend_s.at[0, hop], arecv_s.at[0, hop])
        if hop < half_way:
            await_send(table, asend_l.at[hop], arecv_l.at[hop])
            await_send(table, asend_s.at[1, hop], arecv_s.at[1, hop])


def solution(mesh):
    n = mesh.shape["blk"]
    row_spec = P(("sys", "blk"), None)
    vec_spec = P(("sys", "blk"))

    def local_steps(positions, velocity, charges):
        rows, dim = positions.shape
        hops = n // 4
        pieces = 4 * hops + 1
        dma = pltpu.SemaphoreType.DMA
        whole = pl.BlockSpec(memory_space=pltpu.VMEM)
        flat = jax.ShapeDtypeStruct((rows, dim), F32)
        force_one, pos_two, vel_two, energy = pl.pallas_call(
            functools.partial(kernel, n),
            out_shape=(flat, flat, flat, jax.ShapeDtypeStruct((1,), F32)),
            in_specs=[whole] * 3,
            out_specs=(whole, whole, whole, pl.BlockSpec(memory_space=pltpu.SMEM)),
            scratch_shapes=[
                pltpu.VMEM((2, n, rows, dim), BF16),
                pltpu.VMEM((2, rows, dim), BF16),
                pltpu.VMEM((n, 3, rows // LANES, LANES), F32),
                pltpu.VMEM((2, rows, LANES), F32),
                pltpu.VMEM((rows, LANES), F32),
                pltpu.VMEM((2, rows, dim), F32),
                pltpu.VMEM((2, rows, LANES), F32),
                pltpu.VMEM((n, 8, LANES), F32),
                dma((pieces,)), dma((pieces,)), dma((pieces,)), dma((pieces,)),
                dma((2, pieces)), dma((2, pieces)), dma((2,)), dma((2,)),
                dma((hops + 1,)), dma((hops + 1,)), dma((hops + 1,)), dma((hops + 1,)),
                dma((2, hops + 1)), dma((2, hops + 1)), dma((n,)), dma((n,)),
            ],
            compiler_params=pltpu.CompilerParams(collective_id=0, has_side_effects=True, vmem_limit_bytes=56 << 20),
            name="leapfrog",
        )(positions, velocity, charges.reshape(rows // LANES, LANES))
        return force_one, energy, pos_two, vel_two

    return jax.shard_map(local_steps, mesh=mesh, in_specs=(row_spec, row_spec, vec_spec),
                         out_specs=(row_spec, P("sys"), row_spec, row_spec), check_vma=False)
```

time: 844 us -> 110 us (0.13)
  matrix products: 333 us -> 0 us
  local copies, waits for them, and re-layouts: 114 us -> 4.92 us
  blocking collectives: 104 us -> 0 us
  Pallas kernels: 0 us -> 102 us
  other arithmetic: 96.7 us -> 0 us
  starting transfers between devices: 73.1 us -> 0 us
  loops' own time: 72 us -> 0 us
  waiting for transfers between devices: 41.7 us -> 0 us
    dot_general x196 -> x0, matrix products: 333 us -> none  [the longest x68 134 us: tile_step(): jnp.einsum('id,jd->ij', x_tile, x_b, preferred_element_type=jnp.float32)]
    psum x1 -> x0, blocking collectives: 104 us -> none  [local_steps(): energy_one = lax.psum(energy_local, 'blk').reshape(1)]
    pallas_call x0 -> x1, Pallas kernels: none -> 102 us  [local_steps(): pl.pallas_call(functools.partial(kernel, n), out_shape=(flat, flat, flat,...]
    dynamic_slice x204 -> x0, local copies, waits for them, and re-layouts: 97.9 us -> none  [the longest x68 48.9 us: tile_step(): q_tile = lax.dynamic_slice_in_dim(q_a, row_start, tile_rows, 0)]
    ppermute x47 -> x0, starting transfers between devices: 73.1 us -> none  [the longest x12 22 us: pair_step(): x_seen = lax.ppermute(x_seen, 'blk', next_perm)]
    another operation x20 -> x0, loops' own time: 72 us -> none  [the longest x18 71.2 us: block_pair(): lax.scan(tile_step, start_state, jnp.arange(rows_a // tile_rows))]
    add x98 -> x0, other arithmetic: 61.2 us -> none  [the longest x12 28.9 us: pair_step(): react_run + react_step]
    ppermute x47 -> x0, waiting for transfers between devices: 41.7 us -> none  [the longest x12 39.5 us: pair_step(): q_seen = lax.ppermute(q_seen, 'blk', next_perm)]
  transfers between devices with their start and end apart: 47 -> 0, of which waited for: 13 -> 0; matrix products, arithmetic and copies ran while one was open for 64% -> 0% of each run, Pallas kernels for 0% -> 0%
where the time goes in v1:
time: 110 us
  Pallas kernels  102 us (93%)
  local copies, waits for them, and re-layouts  4.92 us (4%)
  between operations  2.37 us (2%)
    pallas_call x1, Pallas kernels, local_steps(): pl.pallas_call(functools.partial(kernel, n), out_shape=(flat, flat, flat,...  102 us
    unnamed x7, local copies, waits for them, and re-layouts  4.92 us

profile of v1, /device:TPU:21, one launch (start us, length us, event | category | flops | bytes accessed | tf_op | source)
XLA Modules:
  0.0 109.8 jit_solution(13879368806380108835)
XLA Ops:
  0.6 102.5 %leapfrog.1 = (f32[1024,256]{1,0:T(8,128)}, f32[1024,256]{1,0:T(8,128)}, f32[1024,256]{1,0:T(8,128)}, f32[1]{0:T(128)}) custom-call(f32[1024,256]{1,0:T(8,128)} %x0_ref.1, f32[1024,256]{1,0:T(8,128)} %v0_ref.1, f32[8,128]{1,0:T(8,128)} %bitcast.1), custom_call_target="tpu_custom_call" | custom-call | tf_op jit(solution)/shard_map/leapfrog/pallas_call | solution.py:248
  103.1 0.0 copy-start.1
  103.1 2.4 %copy.11 = f32[1024,256]{1,0:T(8,128)} copy(f32[1024,256]{1,0:T(8,128)} %get-tuple-element.16) | data formatting | bytes 2097152
  106.1 0.0 copy-done.1
  106.1 0.0 copy-start
  106.1 1.0 copy.13
  107.1 0.6 copy-done
  107.7 1.0 copy.14
Async XLA Ops:
  103.1 2.9 %copy-start.1 = (f32[1024,256]{1,0:T(8,128)S(1)}, f32[1024,256]{1,0:T(8,128)}, u32[]{:S(2)}) copy-start(f32[1024,256]{1,0:T(8,128)} %get-tuple-element.18) | copy-start | bytes 3145732
  106.1 1.6 %copy-start = (f32[1024,256]{1,0:T(8,128)S(1)}, f32[1024,256]{1,0:T(8,128)}, u32[]{:S(2)}) copy-start(f32[1024,256]{1,0:T(8,128)} %get-tuple-element.19) | copy-start | bytes 3145732

commit v2 on v1

v2 whole, which is shorter than its diff:
```python
import functools

import jax
import jax.numpy as jnp
from jax import lax
from jax.experimental import pallas as pl
from jax.experimental.pallas import tpu as pltpu
from jax.sharding import PartitionSpec as P

MESH = pl.DeviceIdType.MESH
STEP_SIZE = 0.5
LOG2E = 1.4426950408889634
LANES = 128
F32 = jnp.float32
BF16 = jnp.bfloat16


def kernel(n, x0_hbm, v0_hbm, q_hbm, f0_ref, f1_ref, e_ref,
           x0_ref, v0_ref, xg, xl, aux, sc, qc, acc, rho, ebuf, in_sem,
           send_r, recv_r, send_l, recv_l, send_s, recv_s, own_send, own_recv,
           asend_r, arecv_r, asend_l, arecv_l, asend_s, arecv_s, esend, erecv):
    rows, dim = x0_ref.shape
    unit = rows // 2
    sub = rows // 4
    chunks = rows // LANES
    half_way = n // 4
    scale = LOG2E / (2.0 * dim)
    me = lax.axis_index("blk")
    right = lax.rem(me + 2, n)
    left = lax.rem(me + n - 2, n)
    sib = me + 1 - 2 * lax.rem(me, 2)

    def push(ref, send, recv, target):
        pltpu.make_async_remote_copy(src_ref=ref, dst_ref=ref, send_sem=send, recv_sem=recv,
                                     device_id={"blk": target}, device_id_type=MESH).start()

    def await_recv(ref, send, recv):
        pltpu.make_async_remote_copy(src_ref=ref, dst_ref=ref, send_sem=send, recv_sem=recv,
                                     device_id={"blk": sib}, device_id_type=MESH).wait_recv()

    def await_send(ref, send, recv):
        pltpu.make_async_remote_copy(src_ref=ref, dst_ref=ref, send_sem=send, recv_sem=recv,
                                     device_id={"blk": sib}, device_id_type=MESH).wait_send()

    def unit_ref(ev, src, half):
        return xg.at[ev, src, pl.ds(pl.multiple_of(half * unit, unit), unit), :]

    barrier = pltpu.get_barrier_semaphore()
    for peer in (left, right, sib):
        pl.semaphore_signal(barrier, inc=1, device_id={"blk": peer}, device_id_type=MESH)
    loads = [pltpu.make_async_copy(src, dst, in_sem.at[k])
             for k, (src, dst) in enumerate(((q_hbm, aux.at[me, 0]), (v0_hbm, v0_ref), (x0_hbm, x0_ref)))]
    for load in loads:
        load.start()

    loads[0].wait()
    for c in range(chunks):
        qc[c * LANES:(c + 1) * LANES, :] = jnp.broadcast_to(aux[me, 0, c:c + 1, :], (LANES, LANES)).T
    for load in loads[1:]:
        load.wait()

    @pl.loop(0, chunks)
    def _(c):
        rs = pl.ds(pl.multiple_of(c * LANES, LANES), LANES)
        xg[1, me, rs, :] = (x0_ref[rs, :] + STEP_SIZE * v0_ref[rs, :]).astype(BF16)

    @pl.loop(0, chunks)
    def _(c):
        rs = pl.ds(pl.multiple_of(c * LANES, LANES), LANES)
        xg[0, me, rs, :] = x0_ref[rs, :].astype(BF16)

    pl.semaphore_wait(barrier, 3)

    def push_own(v):
        ev, hr = 1 - (v - 1) // 2, (v - 1) % 2
        push(unit_ref(ev, me, hr), send_r.at[v], recv_r.at[v], right)
        push(unit_ref(ev, me, 1 - hr), send_l.at[v], recv_l.at[v], left)

    push_own(1)
    push_own(2)
    push(xg.at[1, me], own_send.at[1], own_recv.at[1], sib)

    @pl.loop(0, chunks)
    def _(c):
        rs = pl.ds(pl.multiple_of(c * LANES, LANES), LANES)
        for ev in (1, 0):
            wide = xg[ev, me, rs, :].astype(F32)
            xl[ev, rs, :] = (wide * 2.0).astype(BF16)
            norm = jnp.broadcast_to(jnp.sum(wide * wide, axis=1, keepdims=True), (LANES, LANES))
            sc[ev, rs, :] = norm
            aux[me, 1 + ev, pl.ds(c, 1), :] = norm.T[0:1, :]

    acc[...] = jnp.zeros_like(acc)
    rho[...] = jnp.zeros_like(rho)
    push(aux.at[me], asend_s.at[0, 0], arecv_s.at[0, 0], sib)
    push(aux.at[me], asend_r.at[1], arecv_r.at[1], right)
    push(aux.at[me], asend_l.at[1], arecv_l.at[1], left)
    push_own(3)
    push_own(4)
    push(xg.at[0, me], own_send.at[0], own_recv.at[0], sib)

    def pair_unit(ev, src, start, width, own):
        xj = xg[ev, src, pl.ds(pl.multiple_of(start, width), width), :]
        base = start // LANES
        if own:
            diff = lax.broadcasted_iota(jnp.int32, (sub, LANES), 0) - lax.broadcasted_iota(jnp.int32, (sub, LANES), 1)
        for r in range(rows // sub):
            rs = pl.ds(r * sub, sub)
            gram = lax.dot_general(xl[ev, rs, :], xj, (((1,), (1,)), ((), ())), preferred_element_type=F32)
            norm_i = sc[ev, rs, :]
            q_i = qc[rs, :]
            low, total = [], None
            for c in range(width // LANES):
                norm_j = aux[src, 1 + ev, pl.ds(base + c, 1), :]
                q_j = aux[src, 0, pl.ds(base + c, 1), :]
                neg = jnp.minimum(gram[:, c * LANES:(c + 1) * LANES] - (norm_i + norm_j), 0.0)
                weight = (q_i * q_j) * jnp.exp2(neg * scale)
                if own:
                    weight = jnp.where(diff == start + (c * LANES - r * sub), 0.0, weight)
                total = weight if total is None else total + weight
                low.append(weight.astype(BF16))
            rho[ev, rs, :] += total
            acc[ev, rs, :] += jnp.dot(jnp.concatenate(low, axis=1), xj, preferred_element_type=F32)

    def pair_two(ev, src_a, start_a, src_b, start_b, width):
        @pl.loop(0, 2)
        def _(j):
            pair_unit(ev, src_a + j * (src_b - src_a), start_a + j * (start_b - start_a), width, False)

    @pl.loop(0, 4)
    def _(j):
        pair_unit(1 - j // 2, me, lax.rem(j, 2) * unit, unit, True)

    await_recv(aux.at[sib], asend_s.at[0, 0], arecv_s.at[0, 0])

    @pl.loop(0, 2)
    def _(j):
        await_recv(xg.at[1 - j, sib], own_send.at[1 - j], own_recv.at[1 - j])
        pair_two(1 - j, sib, 0, sib, unit, unit)

    full = 4 * (half_way - 1)
    part = unit // 2

    def part_ref(src, half, p):
        return xg.at[0, src, pl.ds(pl.multiple_of(half * unit + p * part, part), part), :]

    @pl.loop(1, full + 2)
    def _(v):
        hop = 1 + (v - 1) // 4
        m = lax.rem(v - 1, 4)
        ev = 1 - m // 2
        hr = lax.rem(m, 2)
        hl = 1 - hr
        src_r = lax.rem(me + n - 2 * hop, n)
        src_l = lax.rem(me + 2 * hop, n)
        sib_r = lax.rem(sib + n - 2 * hop, n)
        sib_l = lax.rem(sib + 2 * hop, n)
        onward = (v <= full - 4) | (v == full - 3)
        parted = v == full - 1

        @pl.when(m == 0)
        def _():
            await_recv(aux.at[src_r], asend_r.at[hop], arecv_r.at[hop])
            push(aux.at[src_r], asend_s.at[0, hop], arecv_s.at[0, hop], sib)

            @pl.when(hop < half_way)
            def _():
                push(aux.at[src_r], asend_r.at[hop + 1], arecv_r.at[hop + 1], right)
                await_recv(aux.at[src_l], asend_l.at[hop], arecv_l.at[hop])
                push(aux.at[src_l], asend_s.at[1, hop], arecv_s.at[1, hop], sib)

                @pl.when(hop < half_way - 1)
                def _():
                    push(aux.at[src_l], asend_l.at[hop + 1], arecv_l.at[hop + 1], left)

        def take(k, src, half, send, recv, target):
            await_recv(unit_ref(ev, src, half), send.at[v], recv.at[v])

            @pl.when(onward)
            def _():
                push(unit_ref(ev, src, half), send.at[v + 4], recv.at[v + 4], target)

            @pl.when(parted)
            def _():
                for p in (0, 1):
                    push(part_ref(src, half, p), send.at[v + 4 + p], recv.at[v + 4 + p], target)

            push(unit_ref(ev, src, half), send_s.at[k, v], recv_s.at[k, v], sib)

        take(0, src_r, hr, send_r, recv_r, right)
        take(1, src_l, hl, send_l, recv_l, left)
        pair_two(ev, src_r, hr * unit, src_l, hl * unit, unit)

        @pl.when(m == 0)
        def _():
            await_recv(aux.at[sib_r], asend_s.at[0, hop], arecv_s.at[0, hop])

            @pl.when(hop < half_way)
            def _():
                await_recv(aux.at[sib_l], asend_s.at[1, hop], arecv_s.at[1, hop])

        await_recv(unit_ref(ev, sib_r, hr), send_s.at[0, v], recv_s.at[0, v])
        await_recv(unit_ref(ev, sib_l, hl), send_s.at[1, v], recv_s.at[1, v])
        pair_two(ev, sib_r, hr * unit, sib_l, hl * unit, unit)

    def force(ev, out_ref):
        @pl.loop(0, chunks)
        def _(c):
            rs = pl.ds(pl.multiple_of(c * LANES, LANES), LANES)
            held = jnp.sum(rho[ev, rs, :], axis=1, keepdims=True)
            out_ref[rs, :] = held * xg[ev, me, rs, :].astype(F32) - acc[ev, rs, :]

    ebuf[me] = jnp.broadcast_to(0.5 * jnp.sum(rho[1], keepdims=True), ebuf.shape[1:])
    force(1, f1_ref)

    far = lax.rem(me + 2 * half_way, n)
    far_sib = lax.rem(sib + 2 * half_way, n)

    @pl.loop(0, 2)
    def _(p):
        v = full + 3 + p
        await_recv(part_ref(far, 0, p), send_r.at[v], recv_r.at[v])
        push(part_ref(far, 0, p), send_s.at[0, v], recv_s.at[0, v], sib)
        await_recv(part_ref(far, 1, p), send_l.at[v], recv_l.at[v])
        push(part_ref(far, 1, p), send_s.at[1, v], recv_s.at[1, v], sib)

        @pl.when(p == 0)
        def _():
            @pl.loop(1, n)
            def _(k):
                peer = lax.rem(me + k, n)
                push(ebuf.at[me], esend.at[peer], erecv.at[me], peer)

        pair_two(0, far, p * part, far, unit + p * part, part)
        await_recv(part_ref(far_sib, 0, p), send_s.at[0, v], recv_s.at[0, v])
        await_recv(part_ref(far_sib, 1, p), send_s.at[1, v], recv_s.at[1, v])
        pair_two(0, far_sib, p * part, far_sib, unit + p * part, part)

    force(0, f0_ref)

    @pl.loop(1, n)
    def _(p):
        peer = lax.rem(me + p, n)
        await_recv(ebuf.at[peer], esend.at[peer], erecv.at[peer])
        await_send(ebuf.at[me], esend.at[peer], erecv.at[me])

    e_ref[0] = jnp.sum(jnp.sum(ebuf[...], axis=0)[0:1, 0:1])

    @pl.loop(1, full + 2)
    def _(v):
        piece = unit_ref(0, me, 0)
        await_send(piece, send_r.at[v], recv_r.at[v])
        await_send(piece, send_l.at[v], recv_l.at[v])
        await_send(piece, send_s.at[0, v], recv_s.at[0, v])
        await_send(piece, send_s.at[1, v], recv_s.at[1, v])

    for v in (full + 3, full + 4):
        piece = part_ref(me, 0, 0)
        await_send(piece, send_r.at[v], recv_r.at[v])
        await_send(piece, send_l.at[v], recv_l.at[v])
        await_send(piece, send_s.at[0, v], recv_s.at[0, v])
        await_send(piece, send_s.at[1, v], recv_s.at[1, v])

    for ev in (0, 1):
        await_send(xg.at[ev, me], own_send.at[ev], own_recv.at[ev])
    table = aux.at[me]
    await_send(table, asend_s.at[0, 0], arecv_s.at[0, 0])
    for hop in range(1, half_way + 1):
        await_send(table, asend_r.at[hop], arecv_r.at[hop])
        await_send(table, asend_s.at[0, hop], arecv_s.at[0, hop])
        if hop < half_way:
            await_send(table, asend_l.at[hop], arecv_l.at[hop])
            await_send(table, asend_s.at[1, hop], arecv_s.at[1, hop])


def solution(mesh):
    n = mesh.shape["blk"]
    row_spec = P(("sys", "blk"), None)
    vec_spec = P(("sys", "blk"))

    def local_steps(positions, velocity, charges):
        rows, dim = positions.shape
        hops = n // 4
        pieces = 4 * hops + 1
        dma = pltpu.SemaphoreType.DMA
        whole = pl.BlockSpec(memory_space=pltpu.VMEM)
        flat = jax.ShapeDtypeStruct((rows, dim), F32)
        force_zero, force_one, energy = pl.pallas_call(
            functools.partial(kernel, n),
            out_shape=(flat, flat, jax.ShapeDtypeStruct((1,), F32)),
            in_specs=[pl.BlockSpec(memory_space=pltpu.HBM)] * 3,
            out_specs=(whole, whole, pl.BlockSpec(memory_space=pltpu.SMEM)),
            scratch_shapes=[
                pltpu.VMEM((rows, dim), F32),
                pltpu.VMEM((rows, dim), F32),
                pltpu.VMEM((2, n, rows, dim), BF16),
                pltpu.VMEM((2, rows, dim), BF16),
                pltpu.VMEM((n, 3, rows // LANES, LANES), F32),
                pltpu.VMEM((2, rows, LANES), F32),
                pltpu.VMEM((rows, LANES), F32),
                pltpu.VMEM((2, rows, dim), F32),
                pltpu.VMEM((2, rows, LANES), F32),
                pltpu.VMEM((n, 8, LANES), F32),
                dma((3,)),
                dma((pieces,)), dma((pieces,)), dma((pieces,)), dma((pieces,)),
                dma((2, pieces)), dma((2, pieces)), dma((2,)), dma((2,)),
                dma((hops + 1,)), dma((hops + 1,)), dma((hops + 1,)), dma((hops + 1,)),
                dma((2, hops + 1)), dma((2, hops + 1)), dma((n,)), dma((n,)),
            ],
            compiler_params=pltpu.CompilerParams(collective_id=0, has_side_effects=True, vmem_limit_bytes=40 << 20),
            name="leapfrog",
        )(*(pltpu.with_memory_space_constraint(a, pltpu.HBM) for a in
             (positions, velocity, charges.reshape(rows // LANES, LANES))))
        force_zero, force_one = force_zero / dim, force_one / dim
        vel_one = velocity + STEP_SIZE * force_zero
        pos_two = (positions + STEP_SIZE * velocity) + STEP_SIZE * vel_one
        return force_one, energy, pos_two, vel_one + STEP_SIZE * force_one

    return jax.shard_map(local_steps, mesh=mesh, in_specs=(row_spec, row_spec, vec_spec),
                         out_specs=(row_spec, P("sys"), row_spec, row_spec), check_vma=False)
```

time: 110 us -> 105 us (0.955)
  local copies, waits for them, and re-layouts: 4.92 us -> 0.01 us
  other arithmetic: 0 us -> 1.87 us
    unnamed x7 -> x4, local copies, waits for them, and re-layouts: 4.92 us -> 0.01 us
    add x0 -> x1, other arithmetic: none -> 1.87 us  [local_steps(): return (force_one, energy, pos_two, vel_one + STEP_SIZE * force_one)]
    pallas_call x1, Pallas kernels: 102 us -> 101 us  [local_steps(): pl.pallas_call(functools.partial(kernel, n), out_shape=(flat, flat, jax.S...]
where the time goes in v2:
time: 105 us
  Pallas kernels  101 us (96%)
  between operations  2.41 us (2%)
  other arithmetic  1.87 us (2%)
    pallas_call x1, Pallas kernels, local_steps(): pl.pallas_call(functools.partial(kernel, n), out_shape=(flat, flat, jax.S...  101 us

profile of v2, /device:TPU:21, one launch (start us, length us, event | category | flops | bytes accessed | tf_op | source)
XLA Modules:
  0.0 105.0 jit_solution(4705094245283996439)
XLA Ops:
  0.6 0.0 copy-start
  0.6 0.0 copy-start.1
  0.7 100.7 %leapfrog.1 = (f32[1024,256]{1,0:T(8,128)S(1)}, f32[1024,256]{1,0:T(8,128)S(1)}, f32[1]{0:T(128)}) custom-call(f32[1024,256]{1,0:T(8,128)} %x0_hbm.1, f32[1024,256]{1,0:T(8,128)} %v0_hbm.1, f32[8,128]{1,0:T(8,128)} %bitcast.1), custom_call_target="tpu_custom_call" | custom-call | tf_op jit(solution)/shard_map/leapfrog/pallas_call | solution.py:288
  101.4 0.0 copy-done
  101.4 0.0 copy-done.1
  101.4 1.9 %multiply_add_fusion = (f32[1024,256]{1,0:T(8,128)}, f32[1024,256]{1,0:T(8,128)}, f32[1024,256]{1,0:T(8,128)}) fusion(f32[1024,256]{1,0:T(8,128)S(1)} %get-tuple-element.7, f32[1024,256]{1,0:T(8,128)S(1)} %copy-done.1, f32[1024,256]{1,0:T(8,128)S(1)} %get-tuple-element.9, f32[1024,256]{1,0:T(8,128)S(1)} %copy-done), kind=kLoop, calls=%fused_computation | loop fusion | flops 2359296 | bytes 7340032 | tf_op jit(solution)/shard_map/add | solution.py:317
Async XLA Ops:
  0.6 100.8 %copy-start = (f32[1024,256]{1,0:T(8,128)S(1)}, f32[1024,256]{1,0:T(8,128)}, u32[]{:S(2)}) copy-start(f32[1024,256]{1,0:T(8,128)} %x0_hbm.1) | copy-start | bytes 3145732
  0.6 100.8 %copy-start.1 = (f32[1024,256]{1,0:T(8,128)S(1)}, f32[1024,256]{1,0:T(8,128)}, u32[]{:S(2)}) copy-start(f32[1024,256]{1,0:T(8,128)} %v0_hbm.1) | copy-start | bytes 3145732

commit v3 on v2

v3 whole, which is shorter than its diff:
```python
import functools

import jax
import jax.numpy as jnp
from jax import lax
from jax.experimental import pallas as pl
from jax.experimental.pallas import tpu as pltpu
from jax.sharding import PartitionSpec as P

MESH = pl.DeviceIdType.MESH
STEP_SIZE = 0.5
LOG2E = 1.4426950408889634
LANES = 128
F32 = jnp.float32
BF16 = jnp.bfloat16


def kernel(n, x0_hbm, v0_hbm, q_hbm, f0_ref, f1_ref, e_ref,
           x0_ref, v0_ref, xg, aux, sc, qc, acc, rho, pout, pin, ebuf, in_sem,
           csend, crecv, tsend, trecv, ssend, srecv, own_send, own_recv,
           asend_r, arecv_r, asend_l, arecv_l, asend_s, arecv_s, psend, precv, esend, erecv):
    rows, dim = x0_ref.shape
    unit = rows // 2
    sub = rows // 4
    chunks = rows // LANES
    hops = n // 4 - 1
    scale = 2.0 * LOG2E / (2.0 * dim)
    me = lax.axis_index("blk")
    right = lax.rem(me + 2, n)
    left = lax.rem(me + n - 2, n)
    sib = me + 1 - 2 * lax.rem(me, 2)
    turn = 1 - 2 * lax.rem(me // 2, 2)

    def side(ev):
        return turn * (1 - 2 * ev)

    def away(dev, ev, hop):
        return lax.rem(dev + n - 2 * side(ev) * hop, n)

    def toward(dev, ev, hop):
        return lax.rem(dev + n + 2 * side(ev) * hop, n)

    def push(ref, send, recv, target, dst=None):
        pltpu.make_async_remote_copy(src_ref=ref, dst_ref=ref if dst is None else dst, send_sem=send, recv_sem=recv,
                                     device_id={"blk": target}, device_id_type=MESH).start()

    def await_recv(ref, send, recv):
        pltpu.make_async_remote_copy(src_ref=ref, dst_ref=ref, send_sem=send, recv_sem=recv,
                                     device_id={"blk": sib}, device_id_type=MESH).wait_recv()

    def await_send(ref, send, recv):
        pltpu.make_async_remote_copy(src_ref=ref, dst_ref=ref, send_sem=send, recv_sem=recv,
                                     device_id={"blk": sib}, device_id_type=MESH).wait_send()

    def span(c):
        return pl.ds(pl.multiple_of(c * LANES, LANES), LANES)

    def piece(ev, src, half):
        return xg.at[ev, src, pl.ds(pl.multiple_of(half * unit, unit), unit), :]

    barrier = pltpu.get_barrier_semaphore()
    for peer in (left, right, sib):
        pl.semaphore_signal(barrier, inc=1, device_id={"blk": peer}, device_id_type=MESH)
    loads = [pltpu.make_async_copy(src, dst, in_sem.at[k])
             for k, (src, dst) in enumerate(((q_hbm, aux.at[me, 0]), (v0_hbm, v0_ref), (x0_hbm, x0_ref)))]
    for load in loads:
        load.start()

    loads[0].wait()
    for c in range(chunks):
        qc[0, c * LANES:(c + 1) * LANES, :] = jnp.broadcast_to(aux[me, 0, c:c + 1, :], (LANES, LANES)).T
    for load in loads[1:]:
        load.wait()

    @pl.loop(0, chunks)
    def _(c):
        xg[1, me, span(c), :] = (x0_ref[span(c), :] + STEP_SIZE * v0_ref[span(c), :]).astype(BF16)

    @pl.loop(0, chunks)
    def _(c):
        xg[0, me, span(c), :] = x0_ref[span(c), :].astype(BF16)

    pl.semaphore_wait(barrier, 3)

    def c_push(ev, src, k, half):
        push(piece(ev, src, half), csend.at[ev, k], crecv.at[ev, k], away(me, ev, 1))

    def t_push(ev, src, k, half):
        push(piece(ev, src, half), tsend.at[ev, k], trecv.at[ev, k], toward(me, ev, 1))

    for ev in (1, 0):
        c_push(ev, me, 0, 0)
        push(xg.at[ev, me], own_send.at[ev], own_recv.at[ev], sib)

    @pl.loop(0, chunks)
    def _(c):
        for ev in (1, 0):
            wide = xg[ev, me, span(c), :].astype(F32)
            norm = jnp.broadcast_to(0.5 * jnp.sum(wide * wide, axis=1, keepdims=True), (LANES, LANES))
            sc[ev, 0, span(c), :] = norm
            aux[me, 1 + ev, pl.ds(c, 1), :] = norm.T[0:1, :]

    acc[...] = jnp.zeros_like(acc)
    rho[...] = jnp.zeros_like(rho)
    push(aux.at[me], asend_s.at[0, 0], arecv_s.at[0, 0], sib)
    push(aux.at[me], asend_r.at[1], arecv_r.at[1], right)
    push(aux.at[me], asend_l.at[1], arecv_l.at[1], left)
    for ev in (1, 0):
        c_push(ev, me, 1, 1)
    for half in (0, 1):
        for ev in (1, 0):
            t_push(ev, me, half, half)

    def pair_unit(ev, party, src, half, own=False):
        mine = toward(me, ev, party)
        xj = xg[ev, src, pl.ds(pl.multiple_of(half * unit, unit), unit), :]
        base = half * (unit // LANES)
        charge = party * (1 + ev)
        if own:
            diff = lax.broadcasted_iota(jnp.int32, (sub, LANES), 0) - lax.broadcasted_iota(jnp.int32, (sub, LANES), 1)
        for r in range(rows // sub):
            rs = pl.ds(r * sub, sub)
            gram = lax.dot_general(xg[ev, mine, rs, :], xj, (((1,), (1,)), ((), ())), preferred_element_type=F32)
            norm_i = sc[ev, party, rs, :]
            q_i = qc[charge, rs, :]
            low, total = [], None
            for c in range(unit // LANES):
                norm_j = aux[src, 1 + ev, pl.ds(base + c, 1), :]
                q_j = aux[src, 0, pl.ds(base + c, 1), :]
                neg = jnp.minimum(gram[:, c * LANES:(c + 1) * LANES] - (norm_i + norm_j), 0.0)
                weight = (q_i * q_j) * jnp.exp2(neg * scale)
                if own:
                    weight = jnp.where(diff == half * unit + (c * LANES - r * sub), 0.0, weight)
                total = weight if total is None else total + weight
                low.append(weight.astype(BF16))
            rho[ev, party, rs, :] += total
            acc[ev, party, rs, :] += jnp.dot(jnp.concatenate(low, axis=1), xj, preferred_element_type=F32)

    @pl.loop(0, 4)
    def _(j):
        pair_unit(1 - j // 2, 0, me, lax.rem(j, 2), own=True)

    await_recv(aux.at[sib], asend_s.at[0, 0], arecv_s.at[0, 0])
    for ev in (1, 0):
        await_recv(xg.at[ev, sib], own_send.at[ev], own_recv.at[ev])

    @pl.loop(0, 4)
    def _(j):
        pair_unit(1 - j // 2, 0, sib, lax.rem(j, 2))

    def table_in(hop):
        for k, (step, send, recv, target) in enumerate(((n - 2 * hop, asend_r, arecv_r, right),
                                                        (2 * hop, asend_l, arecv_l, left))):
            src = lax.rem(me + step, n)
            await_recv(aux.at[src], send.at[hop], recv.at[hop])
            push(aux.at[src], asend_s.at[k, hop], arecv_s.at[k, hop], sib)
            if hop < hops:
                push(aux.at[src], send.at[hop + 1], recv.at[hop + 1], target)

    def table_sib(hop):
        for k, step in enumerate((n - 2 * hop, 2 * hop)):
            await_recv(aux.at[lax.rem(sib + step, n)], asend_s.at[k, hop], arecv_s.at[k, hop])

    def c_take(ev, hop, half):
        k = 2 * (hop - 1) + half
        src = away(me, ev, hop)
        await_recv(piece(ev, src, half), csend.at[ev, k], crecv.at[ev, k])
        push(piece(ev, src, half), ssend.at[ev, k], srecv.at[ev, k], sib)

    def c_sib(ev, hop, half):
        k = 2 * (hop - 1) + half
        await_recv(piece(ev, away(sib, ev, hop), half), ssend.at[ev, k], srecv.at[ev, k])

    def t_take(ev, hop, half):
        k = 2 * (hop - 1) + half
        src = toward(me, ev, hop)
        await_recv(piece(ev, src, half), tsend.at[ev, k], trecv.at[ev, k])
        c_push(ev, src, 2 * hop + half, half)

    @pl.loop(0, 2)
    def _(half):
        for ev in (1, 0):
            c_take(ev, 1, half)
            t_push(ev, away(me, ev, 1), 2 + half, half)

        @pl.when(half == 0)
        def _():
            table_in(1)

        @pl.loop(0, 4)
        def _(j):
            @pl.when(j == 2)
            def _():
                for ev in (1, 0):
                    c_sib(ev, 1, half)

                @pl.when(half == 0)
                def _():
                    table_sib(1)

            ev = 1 - lax.rem(j, 2)
            pair_unit(ev, 0, away(me + (j // 2) * (sib - me), ev, 1), half)

    for half in (0, 1):
        for ev in (1, 0):
            t_take(ev, 1, half)
    table_in(2)

    for ev in (1, 0):
        mate = toward(me, ev, 1)

        @pl.loop(0, chunks)
        def _(c):
            sc[ev, 1, span(c), :] = jnp.broadcast_to(aux[mate, 1 + ev, pl.ds(c, 1), :], (LANES, LANES)).T
            qc[1 + ev, span(c), :] = jnp.broadcast_to(aux[mate, 0, pl.ds(c, 1), :], (LANES, LANES)).T

    @pl.loop(0, 16)
    def _(j):
        @pl.when(j == 8)
        def _():
            for ev in (1, 0):
                t_take(ev, 2, 0)

        ev = lax.rem(j, 2)
        half = lax.rem(j // 2, 2)
        who = lax.rem(j // 4, 2)
        pair_unit(ev, 1, away(me + who * (sib - me), ev, j // 8), half)

    for ev in (1, 0):
        t_take(ev, 2, 1)

    last = 2 * hops - 1

    @pl.loop(2, last)
    def _(k):
        hop = 1 + k // 2
        half = lax.rem(k, 2)
        for ev in (1, 0):
            c_take(ev, hop, half)

        @pl.when(k == last - 1)
        def _():
            table_in(3)

        @pl.loop(0, 8)
        def _(j):
            @pl.when(j == 4)
            def _():
                for ev in (1, 0):
                    c_sib(ev, hop, half)

                @pl.when(k == 2)
                def _():
                    table_sib(2)

                @pl.when(k == last - 1)
                def _():
                    table_sib(3)

            ev = 1 - lax.rem(j // 2, 2)
            pair_unit(ev, lax.rem(j, 2), away(me + (j // 4) * (sib - me), ev, hop), half)

    for ev in (1, 0):
        c_take(ev, hops, 1)

    def last_columns(ev, party):
        @pl.loop(0, 2)
        def _(j):
            if party == 1:
                @pl.when(j == 1)
                def _():
                    c_sib(ev, hops, 1)

            pair_unit(ev, party, away(me + j * (sib - me), ev, hops), 1)

    def force(ev, party, c):
        held = jnp.sum(rho[ev, party, span(c), :], axis=1, keepdims=True)
        return held * xg[ev, toward(me, ev, party), span(c), :].astype(F32) - acc[ev, party, span(c), :]

    def part(ref, ev, half):
        return ref.at[ev, pl.ds(half * unit, unit), :]

    def give(ev, half):
        push(part(pout, ev, half), psend.at[ev, half], precv.at[ev, half], toward(me, ev, 1), part(pin, ev, half))

    for ev in (1, 0):
        last_columns(ev, 1)

        @pl.loop(0, chunks)
        def _(c):
            pout[ev, span(c), :] = force(ev, 1, c).astype(BF16)

        give(ev, 0)

    last_columns(1, 0)
    ebuf[me] = jnp.broadcast_to(0.5 * jnp.sum(rho[1, 0] + rho[1, 1], keepdims=True), ebuf.shape[1:])

    @pl.loop(0, chunks)
    def _(c):
        f1_ref[span(c), :] = force(1, 0, c)

    @pl.loop(1, n)
    def _(k):
        peer = lax.rem(me + k, n)
        push(ebuf.at[me], esend.at[peer], erecv.at[me], peer)

    give(1, 1)
    give(0, 1)
    last_columns(0, 0)

    @pl.loop(0, chunks)
    def _(c):
        f0_ref[span(c), :] = force(0, 0, c)

    for half in (0, 1):
        for ev, out_ref in ((1, f1_ref), (0, f0_ref)):
            await_recv(part(pin, ev, half), psend.at[ev, half], precv.at[ev, half])

            @pl.loop(half * (chunks // 2), (half + 1) * (chunks // 2))
            def _(c):
                out_ref[span(c), :] += pin[ev, span(c), :].astype(F32)

    @pl.loop(1, n)
    def _(p):
        peer = lax.rem(me + p, n)
        await_recv(ebuf.at[peer], esend.at[peer], erecv.at[peer])
        await_send(ebuf.at[me], esend.at[peer], erecv.at[me])

    e_ref[0] = jnp.sum(jnp.sum(ebuf[...], axis=0)[0:1, 0:1])

    for ev in (0, 1):
        @pl.loop(0, 2 * hops)
        def _(k):
            await_send(piece(ev, me, 0), csend.at[ev, k], crecv.at[ev, k])
            await_send(piece(ev, me, 0), ssend.at[ev, k], srecv.at[ev, k])

        @pl.loop(0, 2 * hops - 2)
        def _(k):
            await_send(piece(ev, me, 0), tsend.at[ev, k], trecv.at[ev, k])

        await_send(xg.at[ev, me], own_send.at[ev], own_recv.at[ev])
        for half in (0, 1):
            await_send(part(pout, ev, half), psend.at[ev, half], precv.at[ev, half])

    table = aux.at[me]
    await_send(table, asend_s.at[0, 0], arecv_s.at[0, 0])
    for hop in range(1, hops + 1):
        await_send(table, asend_r.at[hop], arecv_r.at[hop])
        await_send(table, asend_l.at[hop], arecv_l.at[hop])
        await_send(table, asend_s.at[0, hop], arecv_s.at[0, hop])
        await_send(table, asend_s.at[1, hop], arecv_s.at[1, hop])


def solution(mesh):
    n = mesh.shape["blk"]
    row_spec = P(("sys", "blk"), None)
    vec_spec = P(("sys", "blk"))

    def local_steps(positions, velocity, charges):
        rows, dim = positions.shape
        hops = n // 4 - 1
        dma = pltpu.SemaphoreType.DMA
        whole = pl.BlockSpec(memory_space=pltpu.VMEM)
        flat = jax.ShapeDtypeStruct((rows, dim), F32)
        force_zero, force_one, energy = pl.pallas_call(
            functools.partial(kernel, n),
            out_shape=(flat, flat, jax.ShapeDtypeStruct((1,), F32)),
            in_specs=[pl.BlockSpec(memory_space=pltpu.HBM)] * 3,
            out_specs=(whole, whole, pl.BlockSpec(memory_space=pltpu.SMEM)),
            scratch_shapes=[
                pltpu.VMEM((rows, dim), F32),
                pltpu.VMEM((rows, dim), F32),
                pltpu.VMEM((2, n, rows, dim), BF16),
                pltpu.VMEM((n, 3, rows // LANES, LANES), F32),
                pltpu.VMEM((2, 2, rows, LANES), F32),
                pltpu.VMEM((3, rows, LANES), F32),
                pltpu.VMEM((2, 2, rows, dim), F32),
                pltpu.VMEM((2, 2, rows, LANES), F32),
                pltpu.VMEM((2, rows, dim), BF16),
                pltpu.VMEM((2, rows, dim), BF16),
                pltpu.VMEM((n, 8, LANES), F32),
                dma((3,)),
                dma((2, 2 * hops)), dma((2, 2 * hops)), dma((2, 2 * hops)), dma((2, 2 * hops)),
                dma((2, 2 * hops)), dma((2, 2 * hops)), dma((2,)), dma((2,)),
                dma((hops + 1,)), dma((hops + 1,)), dma((hops + 1,)), dma((hops + 1,)),
                dma((2, hops + 1)), dma((2, hops + 1)), dma((2, 2)), dma((2, 2)), dma((n,)), dma((n,)),
            ],
            compiler_params=pltpu.CompilerParams(collective_id=0, has_side_effects=True, vmem_limit_bytes=48 << 20),
            name="leapfrog",
        )(*(pltpu.with_memory_space_constraint(a, pltpu.HBM) for a in
            (positions, velocity, charges.reshape(rows // LANES, LANES))))
        force_zero, force_one = force_zero / dim, force_one / dim
        vel_one = velocity + STEP_SIZE * force_zero
        pos_two = (positions + STEP_SIZE * velocity) + STEP_SIZE * vel_one
        return force_one, energy, pos_two, vel_one + STEP_SIZE * force_one

    return jax.shard_map(local_steps, mesh=mesh, in_specs=(row_spec, row_spec, vec_spec),
                         out_specs=(row_spec, P("sys"), row_spec, row_spec), check_vma=False)
```

time: 105 us -> 108 us (1.029)
  Pallas kernels: 101 us -> 103 us
    pallas_call x1, Pallas kernels: 101 us -> 103 us  [local_steps(): pl.pallas_call(functools.partial(kernel, n), out_shape=(flat, flat, jax.S...]
where the time goes in v3:
time: 108 us
  Pallas kernels  103 us (95%)
  between operations  2.41 us (2%)
  other arithmetic  1.87 us (2%)
    pallas_call x1, Pallas kernels, local_steps(): pl.pallas_call(functools.partial(kernel, n), out_shape=(flat, flat, jax.S...  103 us

profile of v3, /device:TPU:21, one launch (start us, length us, event | category | flops | bytes accessed | tf_op | source)
XLA Modules:
  0.0 107.6 jit_solution(15476773501160355698)
XLA Ops:
  0.6 0.0 copy-start
  0.6 0.0 copy-start.1
  0.7 103.3 %leapfrog.1 = (f32[1024,256]{1,0:T(8,128)S(1)}, f32[1024,256]{1,0:T(8,128)S(1)}, f32[1]{0:T(128)}) custom-call(f32[1024,256]{1,0:T(8,128)} %x0_hbm.1, f32[1024,256]{1,0:T(8,128)} %v0_hbm.1, f32[8,128]{1,0:T(8,128)} %bitcast.1), custom_call_target="tpu_custom_call" | custom-call | tf_op jit(solution)/shard_map/leapfrog/pallas_call | solution.py:365
  103.9 0.0 copy-done
  103.9 0.0 copy-done.1
  103.9 1.9 %multiply_add_fusion = (f32[1024,256]{1,0:T(8,128)}, f32[1024,256]{1,0:T(8,128)}, f32[1024,256]{1,0:T(8,128)}) fusion(f32[1024,256]{1,0:T(8,128)S(1)} %get-tuple-element.7, f32[1024,256]{1,0:T(8,128)S(1)} %copy-done.1, f32[1024,256]{1,0:T(8,128)S(1)} %get-tuple-element.9, f32[1024,256]{1,0:T(8,128)S(1)} %copy-done), kind=kLoop, calls=%fused_computation | loop fusion | flops 2359296 | bytes 7340032 | tf_op jit(solution)/shard_map/add | solution.py:395
Async XLA Ops:
  0.6 103.3 %copy-start = (f32[1024,256]{1,0:T(8,128)S(1)}, f32[1024,256]{1,0:T(8,128)}, u32[]{:S(2)}) copy-start(f32[1024,256]{1,0:T(8,128)} %x0_hbm.1) | copy-start | bytes 3145732
  0.6 103.3 %copy-start.1 = (f32[1024,256]{1,0:T(8,128)S(1)}, f32[1024,256]{1,0:T(8,128)}, u32[]{:S(2)}) copy-start(f32[1024,256]{1,0:T(8,128)} %v0_hbm.1) | copy-start | bytes 3145732

commit v4 on v3

--- a/solution.py
+++ b/solution.py
@@ -136,17 +136,17 @@
             rho[ev, party, rs, :] += total
             acc[ev, party, rs, :] += jnp.dot(jnp.concatenate(low, axis=1), xj, preferred_element_type=F32)
 
-    @pl.loop(0, 4)
-    def _(j):
-        pair_unit(1 - j // 2, 0, me, lax.rem(j, 2), own=True)
+    for ev in (1, 0):
+        for half in (0, 1):
+            pair_unit(ev, 0, me, half, own=True)
 
     await_recv(aux.at[sib], asend_s.at[0, 0], arecv_s.at[0, 0])
     for ev in (1, 0):
         await_recv(xg.at[ev, sib], own_send.at[ev], own_recv.at[ev])
 
-    @pl.loop(0, 4)
-    def _(j):
-        pair_unit(1 - j // 2, 0, sib, lax.rem(j, 2))
+    for ev in (1, 0):
+        for half in (0, 1):
+            pair_unit(ev, 0, sib, half)
 
     def table_in(hop):
         for k, (step, send, recv, target) in enumerate(((n - 2 * hop, asend_r, arecv_r, right),
@@ -187,19 +187,18 @@
         def _():
             table_in(1)
 
-        @pl.loop(0, 4)
-        def _(j):
-            @pl.when(j == 2)
-            def _():
-                for ev in (1, 0):
-                    c_sib(ev, 1, half)
-
-                @pl.when(half == 0)
-                def _():
-                    table_sib(1)
-
-            ev = 1 - lax.rem(j, 2)
-            pair_unit(ev, 0, away(me + (j // 2) * (sib - me), ev, 1), half)
+        for ev in (1, 0):
+            pair_unit(ev, 0, away(me, ev, 1), half)
+
+        for ev in (1, 0):
+            c_sib(ev, 1, half)
+
+        @pl.when(half == 0)
+        def _():
+            table_sib(1)
+
+        for ev in (1, 0):
+            pair_unit(ev, 0, away(sib, ev, 1), half)
 
     for half in (0, 1):
         for ev in (1, 0):
@@ -214,17 +213,17 @@
             sc[ev, 1, span(c), :] = jnp.broadcast_to(aux[mate, 1 + ev, pl.ds(c, 1), :], (LANES, LANES)).T
             qc[1 + ev, span(c), :] = jnp.broadcast_to(aux[mate, 0, pl.ds(c, 1), :], (LANES, LANES)).T
 
-    @pl.loop(0, 16)
+    @pl.loop(0, 4)
     def _(j):
-        @pl.when(j == 8)
+        @pl.when(j == 2)
         def _():
             for ev in (1, 0):
                 t_take(ev, 2, 0)
 
-        ev = lax.rem(j, 2)
-        half = lax.rem(j // 2, 2)
-        who = lax.rem(j // 4, 2)
-        pair_unit(ev, 1, away(me + who * (sib - me), ev, j // 8), half)
+        who = lax.rem(j, 2)
+        for ev in (1, 0):
+            for half in (0, 1):
+                pair_unit(ev, 1, away(me + who * (sib - me), ev, j // 2), half)
 
     for ev in (1, 0):
         t_take(ev, 2, 1)
@@ -242,9 +241,9 @@
         def _():
             table_in(3)
 
-        @pl.loop(0, 8)
+        @pl.loop(0, 2)
         def _(j):
-            @pl.when(j == 4)
+            @pl.when(j == 1)
             def _():
                 for ev in (1, 0):
                     c_sib(ev, hop, half)
@@ -257,21 +256,12 @@
                 def _():
                     table_sib(3)
 
-            ev = 1 - lax.rem(j // 2, 2)
-            pair_unit(ev, lax.rem(j, 2), away(me + (j // 4) * (sib - me), ev, hop), half)
+            for ev in (1, 0):
+                for party in (1, 0):
+                    pair_unit(ev, party, away(me + j * (sib - me), ev, hop), half)
 
     for ev in (1, 0):
         c_take(ev, hops, 1)
-
-    def last_columns(ev, party):
-        @pl.loop(0, 2)
-        def _(j):
-            if party == 1:
-                @pl.when(j == 1)
-                def _():
-                    c_sib(ev, hops, 1)
-
-            pair_unit(ev, party, away(me + j * (sib - me), ev, hops), 1)
 
     def force(ev, party, c):
         held = jnp.sum(rho[ev, party, span(c), :], axis=1, keepdims=True)
@@ -283,16 +273,26 @@
     def give(ev, half):
         push(part(pout, ev, half), psend.at[ev, half], precv.at[ev, half], toward(me, ev, 1), part(pin, ev, half))
 
-    for ev in (1, 0):
-        last_columns(ev, 1)
-
+    @pl.loop(0, 2)
+    def _(j):
+        @pl.when(j == 1)
+        def _():
+            for ev in (1, 0):
+                c_sib(ev, hops, 1)
+
+        for ev in (1, 0):
+            pair_unit(ev, 1, away(me + j * (sib - me), ev, hops), 1)
+
+    for ev in (1, 0):
         @pl.loop(0, chunks)
         def _(c):
             pout[ev, span(c), :] = force(ev, 1, c).astype(BF16)
 
         give(ev, 0)
 
-    last_columns(1, 0)
+    for dev in (me, sib):
+        pair_unit(1, 0, away(dev, 1, hops), 1)
+
     ebuf[me] = jnp.broadcast_to(0.5 * jnp.sum(rho[1, 0] + rho[1, 1], keepdims=True), ebuf.shape[1:])
 
     @pl.loop(0, chunks)
@@ -306,7 +306,8 @@
 
     give(1, 1)
     give(0, 1)
-    last_columns(0, 0)
+    for dev in (me, sib):
+        pair_unit(0, 0, away(dev, 0, hops), 1)
 
     @pl.loop(0, chunks)
     def _(c):

time: 108 us -> 96.7 us (0.90)
  Pallas kernels: 103 us -> 92.3 us
    pallas_call x1, Pallas kernels: 103 us -> 92.3 us  [local_steps(): pl.pallas_call(functools.partial(kernel, n), out_shape=(flat, flat, jax.S...]
where the time goes in v4:
time: 96.7 us; the launch traced here: 96.6 us
  Pallas kernels  92.3 us (95%)
  between operations  2.41 us (2%)
  other arithmetic  1.87 us (2%)
    pallas_call x1, Pallas kernels, local_steps(): pl.pallas_call(functools.partial(kernel, n), out_shape=(flat, flat, jax.S...  92.3 us

profile of v4, /device:TPU:21, one launch (start us, length us, event | category | flops | bytes accessed | tf_op | source)
XLA Modules:
  0.0 96.6 jit_solution(5182652105696559770)
XLA Ops:
  0.6 0.0 copy-start
  0.6 0.0 copy-start.1
  0.7 92.3 %leapfrog.1 = (f32[1024,256]{1,0:T(8,128)S(1)}, f32[1024,256]{1,0:T(8,128)S(1)}, f32[1]{0:T(128)}) custom-call(f32[1024,256]{1,0:T(8,128)} %x0_hbm.1, f32[1024,256]{1,0:T(8,128)} %v0_hbm.1, f32[8,128]{1,0:T(8,128)} %bitcast.1), custom_call_target="tpu_custom_call" | custom-call | tf_op jit(solution)/shard_map/leapfrog/pallas_call | solution.py:366
  93.0 0.0 copy-done
  93.0 0.0 copy-done.1
  93.0 1.9 %multiply_add_fusion = (f32[1024,256]{1,0:T(8,128)}, f32[1024,256]{1,0:T(8,128)}, f32[1024,256]{1,0:T(8,128)}) fusion(f32[1024,256]{1,0:T(8,128)S(1)} %get-tuple-element.7, f32[1024,256]{1,0:T(8,128)S(1)} %copy-done.1, f32[1024,256]{1,0:T(8,128)S(1)} %get-tuple-element.9, f32[1024,256]{1,0:T(8,128)S(1)} %copy-done), kind=kLoop, calls=%fused_computation | loop fusion | flops 2359296 | bytes 7340032 | tf_op jit(solution)/shard_map/add | solution.py:396
Async XLA Ops:
  0.6 92.4 %copy-start = (f32[1024,256]{1,0:T(8,128)S(1)}, f32[1024,256]{1,0:T(8,128)}, u32[]{:S(2)}) copy-start(f32[1024,256]{1,0:T(8,128)} %x0_hbm.1) | copy-start | bytes 3145732
  0.6 92.4 %copy-start.1 = (f32[1024,256]{1,0:T(8,128)S(1)}, f32[1024,256]{1,0:T(8,128)}, u32[]{:S(2)}) copy-start(f32[1024,256]{1,0:T(8,128)} %v0_hbm.1) | copy-start | bytes 3145732
